TPU v7x, 256 devices: a whole 4x4x8 slice. The times are simulated.
256 devices in a mesh: row: 32 (over z_lo, y, core), col: 8 (over x, z_hi).
Axes of the slice: x: 4, y: 4, z: 8 (z_hi: 2, z_lo: 4; z = z_hi * 4 + z_lo), core: 2. Of those that a mesh axis runs over, the one named last changes fastest.
Arguments:
- pair_rep: bfloat16 [2048, 2048, 128], P('row', 'col'), may hold values from -6 to 6
- bias_weight: bfloat16 [128, 12], replicated, may hold values from -0.5 to 0.5
- head_weight: float32 [12], replicated, may hold values from -1 to 1
- queries: float32 [192, 2048], P(None, 'row'), may hold values from -48 to 48, as said below
- key_vectors: float32 [192, 2048], P(None, 'col'), may hold values from -48 to 48, as said below
- values: float32 [192, 2048], P(None, 'col'), may hold values from -6 to 6
- query_points: float32 [3, 48, 2048], P(None, None, 'row'), may hold values from -6 to 6
- key_points: float32 [3, 48, 2048], P(None, None, 'col'), may hold values from -6 to 6
- value_points: float32 [3, 96, 2048], P(None, None, 'col'), may hold values from -6 to 6
- rotations: float32 [3, 3, 2048], replicated, may hold values from -1 to 1, as said below
- translations: float32 [3, 2048], replicated, may hold values from -12 to 12
- residue_count: int32 [1], replicated, may hold values from 1024 to 2048
- grad_output: float32 [192, 2048], P(None, 'row'), may hold values from -6 to 6
- grad_points: float32 [3, 96, 2048], P(None, None, 'row'), may hold values from -6 to 6
- grad_pair: bfloat16 [2048, 12, 128], P('row'), may hold values from -2 to 2
Outputs:
- pair_grad: bfloat16 [2048, 2048, 128], P('row', 'col')
- query_grad: float32 [192, 2048], P(None, ('row', 'col'))
- query_point_grad: float32 [3, 48, 2048], P(None, None, ('row', 'col'))
- query_frame_grad: float32 [3, 4, 2048], P(None, None, ('row', 'col'))
- key_grad: float32 [192, 2048], P(None, ('col', 'row'))
- value_grad: float32 [192, 2048], P(None, ('col', 'row'))
- key_point_grad: float32 [3, 48, 2048], P(None, None, ('col', 'row'))
- value_point_grad: float32 [3, 96, 2048], P(None, None, ('col', 'row'))
- key_frame_grad: float32 [3, 4, 2048], P(None, None, ('col', 'row'))
- bias_weight_grad: float32 [128, 12], replicated
- head_weight_grad: float32 [12], replicated
Inputs may be any that keep to these rules, and one draw needn't show every extreme that they name: `queries`: entries of order one, except a few residues whose vectors are much larger. `key_vectors`: entries of order one, except a few residues whose vectors are much larger. `rotations`: each residue's 3 x 3 matrix is a rotation: orthonormal with determinant one.
All inputs are finite; a program needn't handle non-finite values.
Results may differ from a plain program's by a relative error of at most 0.0049.
Values sent between devices are 32-bit elements; how exact they have to be, the bound alone decides.
A program may use at most 128 MiB of HBM per device.

v0:
```python
import functools
import math

import jax
import jax.numpy as jnp
from jax import lax
from jax.sharding import Mesh
from jax.sharding import PartitionSpec as P

ROW = ("row_0", "row_1", "row_2")
COL = ("col_0", "col_1")
ROW_COL = ("row_0", "row_1", "row_2", "col_0", "col_1")
COL_ROW = ("col_0", "col_1", "row_0", "row_1", "row_2")


HIGHEST = lax.Precision.HIGHEST


def from_everyone(shard, axis):
    count = lax.axis_size(axis)
    return lax.all_to_all(
        jnp.broadcast_to(shard[None], (count, *shard.shape)), axis, 0, 0, tiled=True
    )


def over_copies(shard, axis):
    return from_everyone(shard, axis).max(axis=0)


def over_copies_2(shard, axis):
    return from_everyone(shard, axis).sum(axis=0)


def packed_total(arrays, axis):
    ends = [0]
    for a in arrays:
        ends.append(ends[-1] + a.size)
    total = over_copies_2(jnp.concatenate([a.ravel() for a in arrays]), axis)
    return tuple((total[b:e].reshape(a.shape) for a, b, e in zip(arrays, ends, ends[1:])))


def split_up(shard, dim, count):
    before, after = (shard.shape[:dim], shard.shape[dim + 1 :])
    return jnp.moveaxis(shard.reshape(*before, count, -1, *after), dim, 0)


def sum_at_owner(shard, axis, dim):
    count = lax.axis_size(axis)
    parts = lax.all_to_all(split_up(shard, dim, count), axis, 0, 0, tiled=True)
    return jnp.sum(parts, axis=0)


def sum_packed(arrays, axis, dims):
    count = lax.axis_size(axis)
    parts = [split_up(a, dim, count) for a, dim in zip(arrays, dims)]
    lines = jnp.concatenate([b.reshape(count, -1) for b in parts], axis=1)
    rows = max(16, -(-lines.shape[1] // 1024) * 8)
    lines = jnp.pad(lines, ((0, 0), (0, rows * 128 - lines.shape[1]))).reshape(-1, 128)
    flat, at, finished = (lax.psum_scatter(lines, axis, tiled=True).reshape(-1), 0, [])
    for b in parts:
        part = b[0]
        finished.append(flat[at : at + part.size].reshape(part.shape))
        at += part.size
    return tuple(finished)


def by_axis(shard, axes):
    return functools.reduce(lax.psum, axes, shard)


def globalize(rotation, offset, local):
    return jnp.einsum("xym,ykm->xkm", rotation, local, precision=HIGHEST) + offset[:, None, :]


def rotate_back(rotation, vector):
    return jnp.einsum("xym,xkm->ykm", rotation, vector, precision=HIGHEST)


def frame_terms(grad_global, local):
    rotation_part = jnp.einsum("xkm,ykm->xym", grad_global, local, precision=HIGHEST)
    return jnp.concatenate([rotation_part, jnp.sum(grad_global, axis=1)[:, None, :]], axis=1)


def output_frame_terms(point_out, offset, cotan_local, grad_rotated):
    rotation_part = jnp.einsum(
        "xkm,ykm->xym", point_out - offset[:, None, :], cotan_local, precision=HIGHEST
    )
    return jnp.concatenate([rotation_part, -jnp.sum(grad_rotated, axis=1)[:, None, :]], axis=1)


def per_device(
    pair_rep,
    bias_weight,
    head_weight,
    queries,
    key_vectors,
    values,
    query_points,
    key_points,
    value_points,
    rotations,
    translations,
    residue_count,
    grad_output,
    grad_points,
    grad_pair,
):
    heads = bias_weight.shape[1]
    width = queries.shape[0] // heads
    qpoints = query_points.shape[1] // heads
    vpoints = value_points.shape[1] // heads
    rows_here = queries.shape[1]
    cols_here = key_vectors.shape[1]
    logit_scale = math.sqrt(1.0 / 3.0)
    point_scale = math.sqrt(2.0 / (9.0 * qpoints))
    inner_scale = 1.0 / math.sqrt(width)
    distance_coef = 0.5 * logit_scale * point_scale * jax.nn.softplus(head_weight)
    row_start = lax.axis_index(ROW) * rows_here
    col_start = lax.axis_index(COL) * cols_here
    rot_rows = lax.dynamic_slice_in_dim(rotations, row_start, rows_here, 2)
    shift_rows = lax.dynamic_slice_in_dim(translations, row_start, rows_here, 1)
    rot_cols = lax.dynamic_slice_in_dim(rotations, col_start, cols_here, 2)
    shift_cols = lax.dynamic_slice_in_dim(translations, col_start, cols_here, 1)
    query_global = globalize(rot_rows, shift_rows, query_points).reshape(
        3, heads, qpoints, rows_here
    )
    key_global = globalize(rot_cols, shift_cols, key_points).reshape(3, heads, qpoints, cols_here)
    value_global = globalize(rot_cols, shift_cols, value_points).reshape(
        3, heads, vpoints, cols_here
    )
    grad_flat = jnp.einsum("xym,ykm->xkm", rot_rows, grad_points, precision=HIGHEST)
    grad_heads = grad_flat.reshape(3, heads, vpoints, rows_here)
    query_heads = queries.reshape(heads, width, rows_here)
    out_heads = grad_output.reshape(heads, width, rows_here)
    key_heads = key_vectors.reshape(heads, width, cols_here)
    value_heads = values.reshape(heads, width, cols_here)
    valid = col_start + lax.iota(jnp.int32, cols_here) < residue_count[0]
    inner = jnp.einsum("hci,hcj->hij", query_heads, key_heads, precision=HIGHEST)
    cross = jnp.einsum("xhpi,xhpj->hij", query_global, key_global, precision=HIGHEST)
    distance = (
        jnp.sum(query_global**2, axis=(0, 2))[:, :, None]
        + jnp.sum(key_global**2, axis=(0, 2))[:, None, :]
        - 2.0 * cross
    )
    bias = jnp.einsum("ijc,ch->hij", pair_rep, bias_weight, preferred_element_type=jnp.float32)
    logits = logit_scale * (inner_scale * inner + bias) - distance_coef[:, None, None] * distance
    logits = jnp.where(valid[None, None, :], logits, jnp.float32(-1000000000.0))
    product = (
        jnp.einsum("hci,hcj->hij", out_heads, value_heads, precision=HIGHEST)
        + jnp.einsum("xhvi,xhvj->hij", grad_heads, value_global, precision=HIGHEST)
        + jnp.einsum("ijc,ihc->hij", pair_rep, grad_pair, preferred_element_type=jnp.float32)
    )
    row_peak = over_copies(jnp.max(logits, axis=2), COL)
    exponent = jnp.exp(logits - row_peak[:, :, None])
    row_total, row_upper, row_points = packed_total(
        (
            jnp.sum(exponent, axis=2),
            jnp.sum(exponent * product, axis=2),
            jnp.einsum("hij,xhvj->xhvi", exponent, value_global, precision=HIGHEST),
        ),
        COL,
    )
    attention = exponent / row_total[:, :, None]
    delta = row_upper / row_total
    point_out = (row_points / row_total[None, :, None, :]).reshape(3, heads * vpoints, rows_here)
    logit_grad = attention * (product - delta[:, :, None])
    grad_rounded = logit_grad.astype(jnp.bfloat16)
    attn_rounded = attention.astype(jnp.bfloat16)
    pair_grad = (
        logit_scale
        * jnp.einsum("hij,ch->ijc", grad_rounded, bias_weight, preferred_element_type=jnp.float32)
        + jnp.einsum("hij,ihc->ijc", attn_rounded, grad_pair, preferred_element_type=jnp.float32)
    ).astype(jnp.bfloat16)
    weight_part = logit_scale * jnp.einsum(
        "ijc,hij->ch", pair_rep, grad_rounded, preferred_element_type=jnp.float32
    )
    distance_part = jnp.sum(logit_grad * distance, axis=(1, 2))
    query_part = (
        logit_scale
        * inner_scale
        * jnp.einsum("hij,hcj->hci", logit_grad, key_heads, precision=HIGHEST)
    )
    row_sum = jnp.sum(logit_grad, axis=2)
    qpoint_part = (
        -2.0
        * distance_coef[None, :, None, None]
        * (
            query_global * row_sum[None, :, None, :]
            - jnp.einsum("hij,xhpj->xhpi", logit_grad, key_global, precision=HIGHEST)
        )
    )
    query_grad, qpoint_sum = (
        sum_at_owner(query_part.reshape(heads * width, rows_here), COL, 1),
        sum_at_owner(qpoint_part.reshape(3, heads * qpoints, rows_here), COL, 2),
    )
    share = rows_here // lax.axis_size(COL)
    share_start = lax.axis_index(COL) * share
    own_start = row_start + share_start
    rot_own = lax.dynamic_slice_in_dim(rotations, own_start, share, 2)
    shift_own = lax.dynamic_slice_in_dim(translations, own_start, share, 1)
    local_own = lax.dynamic_slice_in_dim(query_points, share_start, share, 2)
    cotan_own = lax.dynamic_slice_in_dim(grad_points, share_start, share, 2)
    out_own = lax.dynamic_slice_in_dim(point_out, share_start, share, 2)
    rotated_own = lax.dynamic_slice_in_dim(grad_flat, share_start, share, 2)
    query_point_grad = rotate_back(rot_own, qpoint_sum)
    query_frame_grad = frame_terms(qpoint_sum, local_own) + output_frame_terms(
        out_own, shift_own, cotan_own, rotated_own
    )
    key_part = (
        logit_scale
        * inner_scale
        * jnp.einsum("hij,hci->hcj", logit_grad, query_heads, precision=HIGHEST)
    )
    value_part = jnp.einsum("hij,hci->hcj", attention, out_heads, precision=HIGHEST)
    col_sum = jnp.sum(logit_grad, axis=1)
    kpoint_part = (
        2.0
        * distance_coef[None, :, None, None]
        * (
            jnp.einsum("hij,xhpi->xhpj", logit_grad, query_global, precision=HIGHEST)
            - key_global * col_sum[None, :, None, :]
        )
    ).reshape(3, heads * qpoints, cols_here)
    vpoint_part = jnp.einsum("hij,xhvi->xhvj", attention, grad_heads, precision=HIGHEST).reshape(
        3, heads * vpoints, cols_here
    )
    key_flat = key_part.reshape(heads * width, cols_here)
    value_flat = value_part.reshape(heads * width, cols_here)
    key_grad, value_grad, kpoint_sum, vpoint_sum = sum_packed(
        (key_flat, value_flat, kpoint_part, vpoint_part), ROW, (1, 1, 2, 2)
    )
    kshare = cols_here // lax.axis_size(ROW)
    kshare_start = lax.axis_index(ROW) * kshare
    rot_keys = lax.dynamic_slice_in_dim(rotations, col_start + kshare_start, kshare, 2)
    klocal_own = lax.dynamic_slice_in_dim(key_points, kshare_start, kshare, 2)
    vlocal_own = lax.dynamic_slice_in_dim(value_points, kshare_start, kshare, 2)
    key_point_grad = rotate_back(rot_keys, kpoint_sum)
    value_point_grad = rotate_back(rot_keys, vpoint_sum)
    key_frame_grad = frame_terms(kpoint_sum, klocal_own) + frame_terms(vpoint_sum, vlocal_own)
    weight_total, distance_total = (by_axis(weight_part, ROW_COL), by_axis(distance_part, ROW_COL))
    head_weight_grad = (
        distance_total * (-0.5 * logit_scale * point_scale) * jax.nn.sigmoid(head_weight)
    )
    return (
        pair_grad,
        query_grad,
        query_point_grad,
        query_frame_grad,
        key_grad,
        value_grad,
        key_point_grad,
        value_point_grad,
        key_frame_grad,
        weight_total,
        head_weight_grad,
    )


def solution(mesh):
    finer = Mesh(mesh.devices.reshape(4, 4, 2, 4, 2), ("row_0", "row_1", "row_2", "col_0", "col_1"))
    in_specs = (
        P(ROW, COL, None),
        P(),
        P(),
        P(None, ROW),
        P(None, COL),
        P(None, COL),
        P(None, None, ROW),
        P(None, None, COL),
        P(None, None, COL),
        P(),
        P(),
        P(),
        P(None, ROW),
        P(None, None, ROW),
        P(ROW, None, None),
    )
    out_specs = (
        P(ROW, COL, None),
        P(None, ROW_COL),
        P(None, None, ROW_COL),
        P(None, None, ROW_COL),
        P(None, COL_ROW),
        P(None, COL_ROW),
        P(None, None, COL_ROW),
        P(None, None, COL_ROW),
        P(None, None, COL_ROW),
        P(),
        P(),
    )
    return jax.shard_map(
        per_device, mesh=finer, in_specs=in_specs, out_specs=out_specs, check_vma=False
    )
```

profile of v0, /device:TPU:1, one launch (start us, length us, event | category | flops | bytes accessed | tf_op | source)
XLA Modules:
  0.0 415.0 jit_solution(17823779164322360788)
XLA Ops:
  17.1 2.0 multiply_reduce_fusion.2
  19.6 3.5 fusion.44
  26.2 11.5 %all-to-all-start = ((f32[8,1,768]{2,1,0:T(1,128)}), f32[8,1,768]{2,1,0:T(1,128)S(1)}, u32[]{:S(2)}, u32[]{:S(2)}) async-start(f32[8,1,768]{2,1,0:T(1,128)} %reshape.192), calls=%async_computation | async-start | bytes 49152 | tf_op jit(solution)/shard_map/all_to_all | solution.py:21
  38.7 2.6 fusion.7
  42.5 3.4 fusion.31
  50.1 3.1 fusion.27
  54.5 9.0 %all-to-all-start.1 = ((f32[8,1,19968]{2,1,0:T(1,128)}), f32[8,1,19968]{2,1,0:T(1,128)S(1)}, u32[]{:S(2)}, u32[]{:S(2)}) async-start(f32[8,1,19968]{2,1,0:T(1,128)} %broadcast_in_dim.25), calls=%async_computation.1 | async-start | bytes 1277952 | tf_op jit(solution)/shard_map/all_to_all | solution.py:21
  68.7 10.0 %all-to-all-done.1 = f32[8,1,19968]{2,1,0:T(1,128)S(1)} async-done(((f32[8,1,19968]{2,1,0:T(1,128)}), f32[8,1,19968]{2,1,0:T(1,128)S(1)}, u32[]{:S(2)}, u32[]{:S(2)}) %all-to-all-start.1) | async-done | bytes 639008 | tf_op jit(solution)/shard_map/all_to_all | solution.py:21
  79.3 2.6 multiply_reduce_fusion
  82.5 1.4 fusion.13
  86.8 4.5 %fusion.23 = f32[64,256,128]{2,1,0:T(8,128)} fusion(bf16[12,64,256]{2,1,0:T(8,128)(2,1)S(1)} %convert_element_type.11, bf16[128,12]{0,1:T(8,128)(2,1)S(1)} %copy-done.31), kind=kOutput, calls=%fused_computation.54 | convolution fusion | flops 50331648 | bytes 8784896 | tf_op jit(solution)/shard_map/hij,ch->ijc/dot_general | solution.py:171
  95.7 4.0 all-to-all-start.3
  108.7 4.7 %reshape_reshape.23 = f32[3,96,32,8]{3,2,1,0:T(8,128)} reshape(f32[3,12,8,256]{3,2,1,0:T(8,128)} %copy.473) | data formatting | bytes 589824 | tf_op jit(solution)/shard_map/reshape;reshape | solution.py:44
  113.4 3.1 copy.474
  118.1 13.9 %all-reduce.4 = (f32[128,12]{0,1:T(8,128)S(1)}, f32[12]{0:T(128)S(1)}) all-reduce(f32[128,12]{0,1:T(8,128)S(1)} %copy-done.29, f32[12]{0:T(128)S(1)} %copy-done.33), channel_id=1, replica_groups=mesh['row_0'=4,'row_1'=4,'row_2'=2,'col_0'=4,'col_1'=2] {'row_0'}, use_global_device_ids=true, to_apply=%region_18.19 | all-reduce | flops 1548 | bytes 12384 | tf_op jit(solution)/shard_map/psum | solution.py:68
  132.0 9.0 %all-reduce.3 = (f32[128,12]{0,1:T(8,128)S(1)}, f32[12]{0:T(128)S(1)}) all-reduce(f32[128,12]{0,1:T(8,128)S(1)} %get-tuple-element.99, f32[12]{0:T(128)S(1)} %get-tuple-element.100), channel_id=1, replica_groups=mesh['row_0'=4,'row_1'=4,'row_2'=2,'col_0'=4,'col_1'=2] {'row_1'}, use_global_device_ids=true, to_apply=%region_19.20 | all-reduce | flops 1548 | bytes 12384 | tf_op jit(solution)/shard_map/psum | solution.py:68
  141.0 7.9 %all-reduce.6 = (f32[128,12]{0,1:T(8,128)S(1)}, f32[12]{0:T(128)S(1)}) all-reduce(f32[128,12]{0,1:T(8,128)S(1)} %get-tuple-element.97, f32[12]{0:T(128)S(1)} %get-tuple-element.98), channel_id=1, replica_groups=mesh['row_0'=4,'row_1'=4,'row_2'=2,'col_0'=4,'col_1'=2] {'row_2'}, use_global_device_ids=true, to_apply=%region_20.21 | all-reduce | flops 1548 | bytes 12384 | tf_op jit(solution)/shard_map/psum | solution.py:68
  148.9 9.6 %all-reduce.2 = (f32[128,12]{0,1:T(8,128)S(1)}, f32[12]{0:T(128)S(1)}) all-reduce(f32[128,12]{0,1:T(8,128)S(1)} %get-tuple-element.103, f32[12]{0:T(128)S(1)} %get-tuple-element.104), channel_id=1, replica_groups=mesh['row_0'=4,'row_1'=4,'row_2'=2,'col_0'=4,'col_1'=2] {'col_0'}, use_global_device_ids=true, to_apply=%region_21.22 | all-reduce | flops 1548 | bytes 12384 | tf_op jit(solution)/shard_map/psum | solution.py:68
  158.5 8.4 %all-reduce.5 = (f32[128,12]{0,1:T(8,128)}, f32[12]{0:T(128)S(1)}) all-reduce(f32[128,12]{0,1:T(8,128)S(1)} %get-tuple-element.95, f32[12]{0:T(128)S(1)} %get-tuple-element.96), channel_id=1, replica_groups=mesh['row_0'=4,'row_1'=4,'row_2'=2,'col_0'=4,'col_1'=2] {'col_1'}, use_global_device_ids=true, to_apply=%region_22.23 | all-reduce | flops 1548 | bytes 12384 | tf_op jit(solution)/shard_map/psum | solution.py:68
  166.9 7.4 %add_convert_fusion = bf16[64,256,128]{2,1,0:T(8,128)(2,1)} fusion(f32[64,256,128]{2,1,0:T(8,128)} %fusion.23, bf16[12,64,256]{2,1,0:T(8,128)(2,1)S(1)} %get-tuple-element.110, bf16[64,12,128]{2,0,1:T(8,128)(2,1)S(1)} %copy-done.4), kind=kOutput, calls=%fused_computation | convolution fusion | flops 56623104 | bytes 13172736 | tf_op jit(solution)/shard_map/hij,ihc->ijc/dot_general | solution.py:172
  177.0 6.7 %all-to-all-start.2 = ((f32[8,192,8]{1,2,0:T(8,128)}), f32[8,192,8]{1,2,0:T(8,128)S(1)}, u32[]{:S(2)}, u32[]{:S(2)}) async-start(f32[8,192,8]{1,2,0:T(8,128)} %bitcast.21), calls=%async_computation.2 | async-start | bytes 131072 | tf_op jit(solution)/shard_map/all_to_all | solution.py:49
  183.8 1.5 reduce.8
  187.3 5.6 %all-to-all-done.2 = f32[8,192,8]{1,2,0:T(8,128)S(1)} async-done(((f32[8,192,8]{1,2,0:T(8,128)}), f32[8,192,8]{1,2,0:T(8,128)S(1)}, u32[]{:S(2)}, u32[]{:S(2)}) %all-to-all-start.2) | async-done | bytes 49184 | tf_op jit(solution)/shard_map/all_to_all | solution.py:49
  193.5 206.1 %all-reduce.9.cloned.1.call-done = f32[1792,128]{1,0:T(8,128)} async-done(((f32[1792,128]{1,0:T(8,128)}), f32[1792,128]{1,0:T(8,128)}) %all-reduce.9.cloned.1.call-update) | async-done | bytes 917520
  (208 shorter events, 57.0 us)
Async XLA Ops:
  7.2 16.8 %copy-start = (f32[192,256]{1,0:T(8,128)S(1)}, f32[192,256]{1,0:T(8,128)}, u32[]{:S(2)}) copy-start(f32[192,256]{1,0:T(8,128)} %param.19) | copy-start | bytes 589828
  7.2 12.4 %copy-start.30 = (bf16[128,12]{0,1:T(8,128)(2,1)S(1)}, bf16[128,12]{0,1:T(8,128)(2,1)}, u32[]{:S(2)}) copy-start(bf16[128,12]{0,1:T(8,128)(2,1)} %param.16) | copy-start | bytes 9220
  13.6 10.5 %copy-start.7 = (f32[192,64]{1,0:T(8,128)}, f32[192,64]{1,0:T(8,128)S(1)}, u32[]{:S(2)}) copy-start(f32[192,64]{1,0:T(8,128)S(1)} %copy.420) | copy-start | bytes 147460
  13.9 9.2 %copy-start.25 = (f32[3,256]{0,1:T(8,128)}, f32[3,256]{0,1:T(8,128)S(1)}, u32[]{:S(2)}) copy-start(f32[3,256]{0,1:T(8,128)S(1)} %copy.428) | copy-start | bytes 9220
  19.6 18.1 %copy-start.17 = (f32[3,96,64]{1,2,0:T(8,128)S(1)}, f32[3,96,64]{1,2,0:T(8,128)}, u32[]{:S(2)}) copy-start(f32[3,96,64]{1,2,0:T(8,128)} %param.28) | copy-start | bytes 221188
  19.6 18.8 %copy-start.21 = (f32[3,96,256]{2,1,0:T(8,128)S(1)}, f32[3,96,256]{2,1,0:T(8,128)}, u32[]{:S(2)}) copy-start(f32[3,96,256]{2,1,0:T(8,128)} %param.23) | copy-start | bytes 884740
  23.1 15.6 %copy-start.26 = (f32[3,256]{0,1:T(8,128)S(1)}, f32[3,256]{0,1:T(8,128)}, u32[]{:S(2)}) copy-start(f32[3,256]{0,1:T(8,128)} %copy-done.25) | copy-start | bytes 9220
  23.1 19.4 %copy-start.3 = (bf16[64,12,128]{2,0,1:T(8,128)(2,1)S(1)}, bf16[64,12,128]{2,0,1:T(8,128)(2,1)}, u32[]{:S(2)}) copy-start(bf16[64,12,128]{2,0,1:T(8,128)(2,1)} %param.29) | copy-start | bytes 589828
  26.2 21.5 %all-to-all-start = ((f32[8,1,768]{2,1,0:T(1,128)}), f32[8,1,768]{2,1,0:T(1,128)S(1)}, u32[]{:S(2)}, u32[]{:S(2)}) async-start(f32[8,1,768]{2,1,0:T(1,128)} %reshape.192), calls=%async_computation | async-start | bytes 49152 | tf_op jit(solution)/shard_map/all_to_all | solution.py:21
  38.4 7.5 %copy-start.13 = (f32[3,96,64]{2,1,0:T(8,128)}, f32[3,96,64]{2,1,0:T(8,128)S(1)}, u32[]{:S(2)}) copy-start(f32[3,96,64]{2,1,0:T(8,128)S(1)} %copy.435) | copy-start | bytes 221188
  46.8 17.5 %copy-start.37 = (u32[256]{0:T(256)S(1)}, u32[256]{0:T(256)}, u32[]{:S(2)}) copy-start(u32[256]{0:T(256)} %constant.67) | copy-start | bytes 3076
  47.7 31.4 %copy-start.19 = (f32[192,64]{1,0:T(8,128)}, f32[192,64]{1,0:T(8,128)S(1)}, u32[]{:S(2)}) copy-start(f32[192,64]{1,0:T(8,128)S(1)} %copy.433) | copy-start | bytes 147460
  49.1 30.0 %copy-start.23 = (f32[12,64]{1,0:T(8,128)}, f32[12,64]{1,0:T(8,128)S(1)}, u32[]{:S(2)}) copy-start(f32[12,64]{1,0:T(8,128)S(1)} %reduce_max.19) | copy-start | bytes 9220
  53.2 28.7 %copy-start.8 = (f32[192,64]{1,0:T(8,128)S(1)}, f32[192,64]{1,0:T(8,128)}, u32[]{:S(2)}) copy-start(f32[192,64]{1,0:T(8,128)} %copy-done.7) | copy-start | bytes 147460
  54.5 24.1 %all-to-all-start.1 = ((f32[8,1,19968]{2,1,0:T(1,128)}), f32[8,1,19968]{2,1,0:T(1,128)S(1)}, u32[]{:S(2)}, u32[]{:S(2)}) async-start(f32[8,1,19968]{2,1,0:T(1,128)} %broadcast_in_dim.25), calls=%async_computation.1 | async-start | bytes 1277952 | tf_op jit(solution)/shard_map/all_to_all | solution.py:21
  95.7 81.3 %all-to-all-start.3 = ((f32[8,1,1152]{2,1,0:T(1,128)}), f32[8,1,1152]{2,1,0:T(1,128)}, u32[]{:S(2)}, u32[]{:S(2)}) async-start(f32[8,1,1152]{2,1,0:T(1,128)} %reshape.194), calls=%async_computation.3 | async-start | bytes 73728 | tf_op jit(solution)/shard_map/all_to_all | solution.py:49
  99.7 299.9 %all-reduce.9.cloned.1.call-start = ((), (), s32[]{:S(2)}) async-start(), calls=%async_computation.4 | async-start | bytes 1835008
  116.5 50.4 %copy-start.4 = (bf16[64,12,128]{2,0,1:T(8,128)(2,1)S(1)}, bf16[64,12,128]{2,0,1:T(8,128)(2,1)}, u32[]{:S(2)}) copy-start(bf16[64,12,128]{2,0,1:T(8,128)(2,1)} %param.29) | copy-start | bytes 589828
  166.9 7.5 %copy-start.27 = (f32[3,96,8]{1,0,2:T(4,128)S(1)}, f32[3,96,8]{1,0,2:T(4,128)}, u32[]{:S(2)}) copy-start(f32[3,96,8]{1,0,2:T(4,128)} %copy.460) | copy-start | bytes 27652
  166.9 8.4 %copy-start.36 = (f32[12]{0:T(128)S(1)}, f32[12]{0:T(128)}, u32[]{:S(2)}) copy-start(f32[12]{0:T(128)} %param.17) | copy-start | bytes 148
  166.9 9.0 %copy-start.18 = (f32[12,16,64]{2,1,0:T(8,128)S(1)}, f32[12,16,64]{2,1,0:T(8,128)}, u32[]{:S(2)}) copy-start(f32[12,16,64]{2,1,0:T(8,128)} %fusion.13) | copy-start | bytes 147460
  166.9 18.5 %copy-start.28 = (f32[3,3,8]{0,1,2:T(4,128)S(1)}, f32[3,3,8]{0,1,2:T(4,128)}, u32[]{:S(2)}) copy-start(f32[3,3,8]{0,1,2:T(4,128)} %copy.508) | copy-start | bytes 868
  166.9 240.6 %copy-start.32 = (f32[3,1,8]{2,1,0:T(1,128)S(1)}, f32[3,1,8]{2,1,0:T(1,128)}, u32[]{:S(2)}) copy-start(f32[3,1,8]{2,1,0:T(1,128)} %copy.463) | copy-start | bytes 292
  177.0 15.8 %all-to-all-start.2 = ((f32[8,192,8]{1,2,0:T(8,128)}), f32[8,192,8]{1,2,0:T(8,128)S(1)}, u32[]{:S(2)}, u32[]{:S(2)}) async-start(f32[8,192,8]{1,2,0:T(8,128)} %bitcast.21), calls=%async_computation.2 | async-start | bytes 131072 | tf_op jit(solution)/shard_map/all_to_all | solution.py:49
  (19 other events, 72.9 us)
Sparse Core Ops, SparseCore 0:
  118.2 281.3 all-reduce.8
where the time goes:
time: 418 us; the launch traced here: 415 us
  waiting for transfers between devices  222 us (53%)
  blocking collectives  48.8 us (12%)
  local copies, waits for them, and re-layouts  45.3 us (11%)
  matrix products  42.1 us (10%)
  starting transfers between devices  31.5 us (8%)
  between operations  16.3 us (4%)
  other arithmetic  9.25 us (2%)
    unnamed x2, waiting for transfers between devices  206 us
    psum x5, blocking collectives, by_axis(): return functools.reduce(lax.psum, axes, shard)  48.8 us
    all_to_all x2, starting transfers between devices, from_everyone(): lax.all_to_all(jnp.broadcast_to(shard[None], (count, *shard.shape)), axis...  20.5 us
    unnamed x96, local copies, waits for them, and re-layouts  11.8 us
    all_to_all x2, starting transfers between devices, sum_at_owner(): parts = lax.all_to_all(split_up(shard, dim, count), axis, 0, 0, tiled=True)  10.7 us
    all_to_all x2, waiting for transfers between devices, from_everyone(): lax.all_to_all(jnp.broadcast_to(shard[None], (count, *shard.shape)), axis...  9.97 us
    another operation x6, local copies, waits for them, and re-layouts, split_up(): return jnp.moveaxis(shard.reshape(*before, count, -1, *after), dim, 0)  8.47 us
  transfers between devices with their start and end apart: 5, of which 3 were waited for; matrix products, arithmetic and copies ran while one was open for 11% of the time, Pallas kernels for 0%

commit v1 on v0

v1 whole, which is shorter than its diff:
```python
import functools
import math

import jax
import jax.numpy as jnp
from jax import lax
from jax.experimental import pallas as pl
from jax.experimental.pallas import tpu as pltpu
from jax.sharding import Mesh
from jax.sharding import PartitionSpec as P

ROW = ("row_0", "row_1", "row_2")
COL = ("col_0", "col_1")
ROW_COL = ("row_0", "row_1", "row_2", "col_0", "col_1")
COL_ROW = ("col_0", "col_1", "row_0", "row_1", "row_2")

MESH = pl.DeviceIdType.MESH
HIGHEST = lax.Precision.HIGHEST
F32 = jnp.float32
BF16 = jnp.bfloat16
VMEM = pl.BlockSpec(memory_space=pltpu.VMEM)
ANY = pl.BlockSpec(memory_space=pl.ANY)
SMEM = pl.BlockSpec(memory_space=pltpu.SMEM)

H, C, PQ, PV, CZ = 12, 16, 4, 8, 128
HP = 16
WL = math.sqrt(1.0 / 3.0)
WC = math.sqrt(2.0 / (9.0 * PQ))
WS = 1.0 / math.sqrt(C)

F_PT = H * C
F_N1 = F_PT + 3 * H * PQ
F_N2 = F_N1 + HP
F_ALL = 384
G_PT = H * C
G_END = G_PT + 3 * H * PV
G_ALL = 512


def iota(shape, dim):
    return lax.broadcasted_iota(jnp.int32, shape, dim)


def head_of_feature(r):
    t = r - F_PT
    t = jnp.where(t >= 96, t - 96, jnp.where(t >= 48, t - 48, t))
    head = jnp.where(r < F_PT, r >> 4, t >> 2)
    head = jnp.where(r >= F_N1, r - F_N1, head)
    head = jnp.where(r >= F_N2, r - F_N2, head)
    return jnp.where(r >= F_N2 + HP, 99, head)


def head_of_value_feature(r):
    t = r - G_PT
    t = jnp.where(t >= 192, t - 192, jnp.where(t >= 96, t - 96, t))
    head = jnp.where(r < G_PT, r >> 4, t >> 3)
    return jnp.where(r >= G_END, 99, head)


def split2(x):
    hi = x.astype(BF16)
    return hi, (x - hi.astype(F32)).astype(BF16)


def split3(x):
    hi = x.astype(BF16)
    rest = x - hi.astype(F32)
    mid = rest.astype(BF16)
    return hi, mid, (rest - mid.astype(F32)).astype(BF16)


def mm(a, b):
    return jnp.dot(a, b, preferred_element_type=F32)


def mm_nt(a, b):
    return lax.dot_general(a, b, (((1,), (1,)), ((), ())), preferred_element_type=F32)


def softplus(x):
    return jnp.maximum(x, 0.0) + jnp.log(1.0 + jnp.exp(-jnp.abs(x)))


def coef_column(hw_ref, heads):
    coef = (0.5 * WL * WC) * softplus(hw_ref[...])
    rows = heads.shape[0]
    return jnp.sum(
        jnp.where(heads == iota((rows, H), 1), jnp.broadcast_to(coef, (rows, H)), 0.0),
        axis=1,
        keepdims=True,
    )


def rotate(rot, local, shift=None):
    out = []
    for x in range(3):
        t = rot[x][0] * local[0] + rot[x][1] * local[1] + rot[x][2] * local[2]
        out.append(t if shift is None else t + shift[x])
    return out


def pair_rows(head_rows, lane_block):
    keep = (iota(head_rows.shape, 0) >> 4) == lane_block
    return jnp.where(keep, head_rows, 0.0).astype(BF16)


def tile(k, size):
    return pl.ds(pl.multiple_of(k * size, size), size)


def mega(
    dims,
    pair_hbm,
    bw_ref,
    hw_ref,
    q_ref,
    k_ref,
    v_ref,
    qp_ref,
    kp_ref,
    vp_ref,
    rot_ref,
    tr_ref,
    count_ref,
    go_ref,
    gpt_ref,
    gpair_ref,
    ab_out,
    kfin_ref,
    qfin_ref,
    wfin_ref,
    pair_v,
    qf_s,
    kf_s,
    vf_s,
    gf_s,
    kt_s,
    kcat_s,
    qcat_s,
    vcat_s,
    gcat_s,
    kparts_s,
    vparts_s,
    w_s,
    g_s,
    p_s,
    pr_s,
    rhs_s,
    dh_s,
    dl_s,
    ah_s,
    al_s,
    kout_s,
    qout_s,
    st_s,
    xst_s,
    cst_s,
    zst_s,
    sc_s,
    kc_s,
    ksum_s,
    ky_s,
    kz_s,
    kr_s,
    qx_s,
    qz_s,
    qr_s,
    wm_s,
    wx_s,
    wz_s,
    wc_s,
    wy_s,
    wr_s,
    pair_sem,
    send_sem,
    recv_sem,
):
    nz, ny, nx, ni, nj = dims
    lanes = ni * HP
    groups = lanes // 128
    chunks = lanes // 256
    z, y, c = lax.axis_index("row_0"), lax.axis_index("row_1"), lax.axis_index("row_2")
    x, w = lax.axis_index("col_0"), lax.axis_index("col_1")

    for g in range(groups):
        pltpu.make_async_copy(
            pair_hbm.at[pl.ds(8 * g, 8)], pair_v.at[pl.ds(8 * g, 8)], pair_sem.at[g]
        ).start()

    barrier = pltpu.get_barrier_semaphore()
    peers = [{"row_2": 1 - c}, {"col_1": 1 - w}]
    peers += [{"row_1": lax.rem(y + r, ny)} for r in range(1, ny)]
    peers += [{"row_0": lax.rem(z + r, nz)} for r in range(1, nz)]
    peers += [{"col_0": lax.rem(x + r, nx)} for r in range(1, nx)]
    for peer in peers:
        pl.semaphore_signal(barrier, inc=1, device_id=peer, device_id_type=MESH)

    used = [0]

    def send(src, dst, peer):
        n = used[0]
        used[0] += 1
        copy = pltpu.make_async_remote_copy(
            src_ref=src,
            dst_ref=dst,
            send_sem=send_sem.at[n],
            recv_sem=recv_sem.at[n],
            device_id=peer,
            device_id_type=MESH,
        )
        copy.start()
        return copy

    base = pl.multiple_of((z * ny + y) * 128, 128)

    def own_half(full):
        return jnp.where(c == 1, pltpu.roll(full, 64, 1), full)[:, :ni]

    rot_q = []
    for a in range(3):
        t = own_half(rot_ref[a, :, pl.ds(base, 128)])
        rot_q.append([t[b : b + 1] for b in range(3)])
    t = own_half(tr_ref[:, pl.ds(base, 128)])
    tr_q = [t[a : a + 1] for a in range(3)]
    col = x * 2 + w
    kbase = tile(col, nj)
    rot_k = []
    for a in range(3):
        t = rot_ref[a, :, kbase]
        rot_k.append([t[b : b + 1] for b in range(3)])
    t = tr_ref[:, kbase]
    tr_k = [t[a : a + 1] for a in range(3)]

    norm_sel = ((iota((HP, 48), 1) >> 2) == iota((HP, 48), 0)).astype(F32)
    qg = rotate(rot_q, [qp_ref[b] for b in range(3)], tr_q)
    gg = rotate(rot_q, [gpt_ref[b] for b in range(3)])
    qf_s[0:F_PT] = q_ref[...]
    for a in range(3):
        qf_s[F_PT + 48 * a : F_PT + 48 * (a + 1)] = qg[a]
    qf_s[F_N1:F_N2] = jnp.ones((HP, ni), F32)
    qf_s[F_N2 : F_N2 + HP] = jnp.dot(
        norm_sel, qg[0] * qg[0] + qg[1] * qg[1] + qg[2] * qg[2], precision=HIGHEST
    )
    qf_s[F_N2 + HP :] = jnp.zeros((F_ALL - F_N2 - HP, ni), F32)
    gf_s[0:G_PT] = go_ref[...]
    for a in range(3):
        gf_s[G_PT + 96 * a : G_PT + 96 * (a + 1)] = gg[a]
    gf_s[G_END:] = jnp.zeros((G_ALL - G_END, ni), F32)

    kg = rotate(rot_k, [kp_ref[b] for b in range(3)], tr_k)
    vg = rotate(rot_k, [vp_ref[b] for b in range(3)], tr_k)
    kf_s[0:F_PT] = k_ref[...]
    for a in range(3):
        kf_s[F_PT + 48 * a : F_PT + 48 * (a + 1)] = kg[a]
    kf_s[F_N1:F_N2] = jnp.dot(
        norm_sel, kg[0] * kg[0] + kg[1] * kg[1] + kg[2] * kg[2], precision=HIGHEST
    )
    kf_s[F_N2 : F_N2 + HP] = jnp.ones((HP, nj), F32)
    kf_s[F_N2 + HP :] = jnp.zeros((F_ALL - F_N2 - HP, nj), F32)
    vf_s[0:G_PT] = v_ref[...]
    for a in range(3):
        vf_s[G_PT + 96 * a : G_PT + 96 * (a + 1)] = vg[a]
    vf_s[G_END:] = jnp.zeros((G_ALL - G_END, nj), F32)

    r = iota((F_ALL, 1), 0)
    coef = coef_column(hw_ref, head_of_feature(r))
    scale = jnp.where(r < F_PT, WL * WS, jnp.where(r < F_N1, 2.0 * coef, -coef))
    kt = jnp.transpose(kf_s[...] * scale)
    kt_s[...] = kt
    hi, mid, lo = split3(kt)
    for n, part in enumerate((hi, hi, mid, mid, hi, lo)):
        kcat_s[:, F_ALL * n : F_ALL * (n + 1)] = part
    hi, lo = split2(jnp.transpose(vf_s[...]))
    for n, part in enumerate((hi, hi, lo)):
        vcat_s[:, G_ALL * n : G_ALL * (n + 1)] = part
    kparts_s[0], kparts_s[1] = split2(kf_s[...])
    vparts_s[0], vparts_s[1] = split2(vf_s[G_PT:G_END])

    q_parts = split3(qf_s[...])
    g_parts = split2(gf_s[...])

    def expand(n, _):
        lane = iota((ni, 256), 1)
        e = ((lane >> 4) + n * 16 == iota((ni, 256), 0)).astype(BF16)
        for b in range(F_ALL // 128):
            head = head_of_feature(iota((128, 256), 0) + 128 * b)
            keep = head == (iota((128, 256), 1) & 15)
            hi, mid, lo = [
                jnp.where(keep, mm(part[128 * b : 128 * (b + 1)], e), 0.0).astype(BF16)
                for part in q_parts
            ]
            for m, part in enumerate((hi, mid, hi, mid, lo, hi)):
                at = F_ALL * m + 128 * b
                qcat_s[at : at + 128, tile(n, 256)] = part
        for b in range(G_ALL // 128):
            head = head_of_value_feature(iota((128, 256), 0) + 128 * b)
            keep = head == (iota((128, 256), 1) & 15)
            hi, lo = [
                jnp.where(keep, mm(part[128 * b : 128 * (b + 1)], e), 0.0).astype(BF16)
                for part in g_parts
            ]
            for m, part in enumerate((hi, lo, hi)):
                at = G_ALL * m + 128 * b
                gcat_s[at : at + 128, tile(n, 256)] = part
        return 0

    lax.fori_loop(0, chunks, expand, 0)

    w_s[...] = jnp.zeros((128, 128), F32)
    w_s[:, 0:H] = bw_ref[...].astype(F32)
    wt = jnp.transpose(w_s[...])[0:HP]
    g_s[...] = jnp.zeros((ni, HP, 128), F32)
    g_s[:, 0:H, :] = gpair_ref[...].astype(F32)
    w_rows = jnp.concatenate([wt] * 8, axis=0)
    for b in range(8):
        rhs_s[0:128, 128 * b : 128 * (b + 1)] = pair_rows(w_rows, b)

    count = count_ref[0]

    def forward(n, _):
        logits = mm(kcat_s[...], qcat_s[:, tile(n, 256)])
        prod = mm(vcat_s[...], gcat_s[:, tile(n, 256)])
        biases, prods = [], []
        for half in range(2):
            g = 2 * n + half
            pltpu.make_async_copy(
                pair_hbm.at[pl.ds(8 * g, 8)], pair_v.at[pl.ds(8 * g, 8)], pair_sem.at[g]
            ).wait()
            g_rows = g_s[pl.ds(8 * g, 8)].reshape(128, 128)
            for b in range(8):
                rhs_s[128:256, 128 * b : 128 * (b + 1)] = pair_rows(g_rows, b)
            acc = None
            for b in range(4):
                two = jnp.concatenate([pair_v[8 * g + 2 * b], pair_v[8 * g + 2 * b + 1]], axis=1)
                part = mm_nt(two, rhs_s[:, 256 * b : 256 * (b + 1)])
                acc = part if acc is None else acc + part
            biases.append(acc[:, :128])
            prods.append(acc[:, 128:])
        logits = logits + WL * jnp.concatenate(biases, axis=1)
        prod = prod + jnp.concatenate(prods, axis=1)
        valid = iota((nj, 256), 0) + col * nj < count
        logits = jnp.where(valid, logits, -1000000000.0)
        peak = jnp.max(logits, axis=0, keepdims=True)
        e = jnp.exp(logits - peak)
        p_s[:, tile(n, 256)] = e
        pr_s[:, tile(n, 256)] = prod
        total = jnp.sum(e, axis=0, keepdims=True)
        upper = jnp.sum(e * prod, axis=0, keepdims=True)
        for half in range(2):
            at = slice(128 * half, 128 * (half + 1))
            st_s[0, pl.ds(2 * n + half, 1), :] = peak[:, at]
            st_s[1, pl.ds(2 * n + half, 1), :] = total[:, at]
            st_s[2, pl.ds(2 * n + half, 1), :] = upper[:, at]
        return 0

    lax.fori_loop(0, chunks, forward, 0)

    pl.semaphore_wait(barrier, len(peers))
    copies = [send(st_s, xst_s.at[r - 1], {"col_0": lax.rem(x + r, nx)}) for r in range(1, nx)]
    for copy in copies:
        copy.wait()
    sets = [(st_s[0], st_s[1], st_s[2])]
    sets += [(xst_s[r, 0], xst_s[r, 1], xst_s[r, 2]) for r in range(nx - 1)]

    def merge(sets):
        peak = functools.reduce(jnp.maximum, [s[0] for s in sets])
        weights = [jnp.exp(s[0] - peak) for s in sets]
        total = sum(s[1] * f for s, f in zip(sets, weights))
        upper = sum(s[2] * f for s, f in zip(sets, weights))
        return peak, total, upper

    mine = merge(sets)
    for a in range(3):
        cst_s[a] = mine[a]
    send(cst_s, zst_s, {"col_1": 1 - w}).wait()
    peak, total, upper = merge([mine, (zst_s[0], zst_s[1], zst_s[2])])
    sc_s[0] = jnp.exp(st_s[0] - peak) / total
    sc_s[1] = upper / total

    def weights_of(g, acc):
        attn = p_s[:, tile(g, 128)] * sc_s[0, pl.ds(g, 1), :]
        dlog = attn * (pr_s[:, tile(g, 128)] - sc_s[1, pl.ds(g, 1), :])
        dh_s[:, tile(g, 128)], dl_s[:, tile(g, 128)] = split2(dlog)
        a_hi, a_lo = split2(attn)
        ah_s[:, tile(g, 128)] = a_hi
        al_s[:, tile(g, 128)] = a_lo
        scaled = WL * dlog
        ab_out[:, pl.ds(pl.multiple_of(g * 256, 256), 128)] = scaled.astype(BF16)
        ab_out[:, pl.ds(pl.multiple_of(g * 256 + 128, 128), 128)] = a_hi
        turned = jnp.transpose(scaled).astype(BF16)
        for b in range(8):
            acc = acc + mm(turned[16 * b : 16 * (b + 1)], pair_v[8 * g + b])
        return acc

    weight = lax.fori_loop(0, groups, weights_of, jnp.zeros((HP, 128), F32))

    kout = mm_nt(dh_s[...], qcat_s[0:F_ALL])
    kout += mm_nt(dh_s[...], qcat_s[F_ALL : 2 * F_ALL])
    kout += mm_nt(dl_s[...], qcat_s[0:F_ALL])
    aout = mm_nt(ah_s[...], gcat_s[0:G_ALL])
    aout += mm_nt(ah_s[...], gcat_s[G_ALL : 2 * G_ALL])
    aout += mm_nt(al_s[...], gcat_s[0:G_ALL])
    slab = nj // (nz * ny * 2)
    kout_s[:, :, :, 0:F_ALL] = kout.reshape(nz * ny, 2, slab, F_ALL)
    kout_s[:, :, :, F_ALL:] = aout.reshape(nz * ny, 2, slab, G_ALL)
    core_copy = send(kout_s.at[:, 1 - c], kc_s, {"row_2": 1 - c})
    spread = jnp.sum(kt_s[...] * kout, axis=0, keepdims=True)

    wm_s[0:H] = weight[0:H]
    wm_s[H : H + 1] = spread[:, 128:256]
    wm_s[H + 1 : H + 2] = spread[:, 256:384]
    wm_s[H + 2 :] = jnp.zeros((HP - H - 2, 128), F32)

    def share(src, slots, axis, me, count):
        slots[me] = src[...]
        return [send(src, slots.at[me], {axis: lax.rem(me + r, count)}) for r in range(1, count)]

    def settle(copies, slots, dst, count):
        for copy in copies:
            copy.wait()
        dst[...] = functools.reduce(lambda a, b: a + b, [slots[n] for n in range(count)])

    wx_copies = share(wm_s, wx_s, "col_0", x, nx)

    def query_side(n, acc):
        at = tile(n, 256)
        lane = iota((ni, 256), 1)
        e = ((lane >> 4) + n * 16 == iota((ni, 256), 0)).astype(BF16)
        outs = []
        for parts, hi_ref, lo_ref, head_of, rows, first in (
            (kparts_s, dh_s, dl_s, head_of_feature, F_ALL, 0),
            (vparts_s, ah_s, al_s, head_of_value_feature, G_END - G_PT, G_PT),
        ):
            full = mm(parts[0], hi_ref[:, at]) + mm(parts[0], lo_ref[:, at])
            full += mm(parts[1], hi_ref[:, at])
            keep = head_of(iota((rows, 256), 0) + first) == (iota((rows, 256), 1) & 15)
            hi, lo = split2(jnp.where(keep, full, 0.0))
            outs.append(mm_nt(e, hi) + mm_nt(e, lo))
        return acc[0] + outs[0], acc[1] + outs[1]

    q1, q2 = lax.fori_loop(
        0,
        chunks,
        query_side,
        (jnp.zeros((ni, F_ALL), F32), jnp.zeros((ni, G_END - G_PT), F32)),
    )
    qslab = ni // (nx * 2)
    qout_s[:, :, :, 0:F_ALL] = q1.reshape(nx, 2, qslab, F_ALL)
    qout_s[:, :, :, F_ALL : F_ALL + G_END - G_PT] = q2.reshape(nx, 2, qslab, G_END - G_PT)
    qout_s[:, :, :, F_ALL + G_END - G_PT :] = jnp.zeros(
        (nx, 2, qslab, qout_s.shape[3] - F_ALL - G_END + G_PT), F32
    )
    qx_copies = []
    for r in range(1, nx):
        peer = lax.rem(x + r, nx)
        qx_copies.append(send(qout_s.at[peer], qx_s.at[r - 1], {"col_0": peer}))

    core_copy.wait()
    ksum_s[...] = (kout_s[:, c] + kc_s[...]).reshape(ksum_s.shape)
    ky_copies = []
    for r in range(1, ny):
        peer = lax.rem(y + r, ny)
        ky_copies.append(send(ksum_s.at[:, peer], ky_s.at[r - 1], {"row_1": peer}))

    settle(wx_copies, wx_s, wm_s, nx)
    wz_copy = send(wm_s, wz_s, {"col_1": 1 - w})
    for copy in qx_copies:
        copy.wait()
    qz_s[...] = functools.reduce(lambda a, b: a + b, [qx_s[r] for r in range(nx - 1)], qout_s[x])
    qz_copy = send(qz_s.at[1 - w], qr_s, {"col_1": 1 - w})

    for copy in ky_copies:
        copy.wait()
    kz_s[...] = functools.reduce(lambda a, b: a + b, [ky_s[r] for r in range(ny - 1)], ksum_s[:, y])
    kz_copies = []
    for r in range(1, nz):
        peer = lax.rem(z + r, nz)
        kz_copies.append(send(kz_s.at[peer], kr_s.at[r - 1], {"row_0": peer}))

    wz_copy.wait()
    wm_s[...] = wm_s[...] + wz_s[...]
    wc_copy = send(wm_s, wc_s, {"row_2": 1 - c})
    wc_copy.wait()
    wm_s[...] = wm_s[...] + wc_s[...]
    wy_copies = share(wm_s, wy_s, "row_1", y, ny)
    qz_copy.wait()
    qfin_ref[...] = qz_s[w] + qr_s[...]
    settle(wy_copies, wy_s, wm_s, ny)
    wr_copies = share(wm_s, wr_s, "row_0", z, nz)
    for copy in kz_copies:
        copy.wait()
    kfin_ref[...] = functools.reduce(lambda a, b: a + b, [kr_s[r] for r in range(nz - 1)], kz_s[z])
    settle(wr_copies, wr_s, wfin_ref, nz)


def finish(
    dims,
    ab_ref,
    gpair_ref,
    bw_ref,
    hw_ref,
    kfin_ref,
    qfin_ref,
    wfin_ref,
    qp_ref,
    kp_ref,
    vp_ref,
    rot_ref,
    tr_ref,
    gpt_ref,
    pair_out,
    q_out,
    qp_out,
    qf_out,
    k_out,
    v_out,
    kp_out,
    vp_out,
    kf_out,
    w_out,
    hw_out,
    g_s,
    w_s,
    t_s,
    tq_s,
    rhs_s,
):
    nz, ny, nx, ni, nj = dims
    z, y, c = lax.axis_index("row_0"), lax.axis_index("row_1"), lax.axis_index("row_2")
    x, w = lax.axis_index("col_0"), lax.axis_index("col_1")
    row = (z * ny + y) * 2 + c
    col = x * 2 + w
    slab = nj // (nz * ny * 2)
    qslab = ni // (nx * 2)

    @pl.when(pl.program_id(0) == 0)
    def _():
        w_s[...] = jnp.zeros((128, 128), F32)
        w_s[:, 0:H] = bw_ref[...].astype(F32)
        w_rows = jnp.concatenate([jnp.transpose(w_s[...])[0:HP]] * 8, axis=0)
        for b in range(8):
            rhs_s[0:128, 128 * b : 128 * (b + 1)] = pair_rows(w_rows, b)
        g_s[...] = jnp.zeros(g_s.shape, F32)

    g_s[:, 0:H, :] = gpair_ref[...].astype(F32)
    g_rows = g_s[...].reshape(128, 128)
    for b in range(8):
        rhs_s[128:256, 128 * b : 128 * (b + 1)] = pair_rows(g_rows, b)
    for b in range(4):
        two = mm(ab_ref[...], rhs_s[:, 256 * b : 256 * (b + 1)]).astype(BF16)
        pair_out[2 * b] = two[:, :128]
        pair_out[2 * b + 1] = two[:, 128:]

    @pl.when(pl.program_id(0) == 0)
    def _():
        def pick(count, start):
            return (iota((count, 128), 0) == start + iota((count, 128), 1)).astype(F32)

        def exact(a, b):
            return jnp.dot(a, b, precision=HIGHEST)

        def split_rows(t):
            return [t[b : b + 1] for b in range(3)]

        expand = ((iota((48, HP), 0) >> 2) == iota((48, HP), 1)).astype(F32)
        coef = coef_column(hw_ref, iota((48, 1), 0) >> 2)

        at = row * slab
        sel = pick(128, lax.rem(at, 128))
        base = tile(col * (nj // 128) + at // 128, 128)
        here = tile(at // 128, 128)
        rot = [split_rows(exact(rot_ref[a, :, base], sel)) for a in range(3)]
        shift = split_rows(exact(tr_ref[:, base], sel))
        kp = [exact(kp_ref[b, :, here], sel) for b in range(3)]
        vp = [exact(vp_ref[b, :, here], sel) for b in range(3)]
        kg = rotate(rot, kp, shift)
        t_s[...] = jnp.zeros(t_s.shape, F32)
        t_s[0:slab] = kfin_ref[...]
        kt = jnp.transpose(t_s[...])
        k_out[...] = (WL * WS) * kt[0:F_PT, :slab]
        v_out[...] = kt[F_ALL : F_ALL + G_PT, :slab]
        sums = exact(expand, kt[F_N1:F_N2])
        dkg = [
            2.0 * coef * (kt[F_PT + 48 * a : F_PT + 48 * (a + 1)] - kg[a] * sums) for a in range(3)
        ]
        v_at = F_ALL + G_PT
        dvg = [kt[v_at + 96 * a : v_at + 96 * (a + 1)] for a in range(3)]
        for b in range(3):
            kp_out[b] = (rot[0][b] * dkg[0] + rot[1][b] * dkg[1] + rot[2][b] * dkg[2])[:, :slab]
            vp_out[b] = (rot[0][b] * dvg[0] + rot[1][b] * dvg[1] + rot[2][b] * dvg[2])[:, :slab]

        def over(t):
            return jnp.sum(t, axis=0, keepdims=True)

        for a in range(3):
            for b in range(3):
                kf_out[a, b : b + 1] = (over(dkg[a] * kp[b]) + over(dvg[a] * vp[b]))[:, :slab]
            kf_out[a, 3:4] = (over(dkg[a]) + over(dvg[a]))[:, :slab]

        inner = c * ni + col * qslab
        sel = pick(128, inner)
        base = tile(z * ny + y, 128)
        rot = [split_rows(exact(rot_ref[a, :, base], sel)) for a in range(3)]
        shift = split_rows(exact(tr_ref[:, base], sel))
        sel = pick(ni, col * qslab)
        qp = [exact(qp_ref[b], sel) for b in range(3)]
        gp = [exact(gpt_ref[b], sel) for b in range(3)]
        qg = rotate(rot, qp, shift)
        gg = rotate(rot, gp)
        tq_s[...] = jnp.zeros(tq_s.shape, F32)
        tq_s[0:qslab] = qfin_ref[...]
        qt = jnp.transpose(tq_s[...])
        q_out[...] = (WL * WS) * qt[0:F_PT, :qslab]
        sums = exact(expand, qt[F_N2 : F_N2 + HP])
        dqg = [
            -2.0 * coef * (qg[a] * sums - qt[F_PT + 48 * a : F_PT + 48 * (a + 1)]) for a in range(3)
        ]
        opt = [qt[F_ALL + 96 * a : F_ALL + 96 * (a + 1)] - shift[a] for a in range(3)]
        for b in range(3):
            qp_out[b] = (rot[0][b] * dqg[0] + rot[1][b] * dqg[1] + rot[2][b] * dqg[2])[:, :qslab]
        for a in range(3):
            for b in range(3):
                qf_out[a, b : b + 1] = (over(dqg[a] * qp[b]) + over(opt[a] * gp[b]))[:, :qslab]
            qf_out[a, 3:4] = (over(dqg[a]) - over(gg[a]))[:, :qslab]

        w_s[...] = jnp.zeros((128, 128), F32)
        w_s[0:HP] = wfin_ref[...]
        w_out[...] = jnp.transpose(w_s[...])[:, 0:H]
        total = jnp.zeros((1, 128), F32)
        for n in range(2):
            f = iota((128, 128), 0) + 128 * (n + 1)
            keep = (head_of_feature(f) == iota((128, 128), 1)) & (f >= F_PT)
            total += exact(wfin_ref[H + n : H + n + 1], keep.astype(F32))
        hw = hw_ref[...]
        hw_out[...] = total[:, 0:H] / (softplus(hw) * (1.0 + jnp.exp(-hw)))


def per_device(dims, *args):
    (pair, bw, hw, q, k, v, qp, kp, vp, rot, tr, count, go, gpt, gpair) = args
    nz, ny, nx, ni, nj = dims
    hw = hw.reshape(1, H)
    lanes = ni * HP
    slab, qslab = nj // (nz * ny * 2), ni // (nx * 2)
    kw, qw = F_ALL + G_ALL, 768
    groups = lanes // 128
    sends = 2 * ((nx - 1) + 1) + 1 + (ny - 1) + (nz - 1) + (nx - 1) + 1 + 1 + (ny - 1) + (nz - 1)

    def buf(*shape, dtype=F32):
        return pltpu.VMEM(shape, dtype)

    ab, kfin, qfin, wfin = pl.pallas_call(
        functools.partial(mega, dims),
        out_shape=[
            jax.ShapeDtypeStruct((nj, 2 * lanes), BF16),
            jax.ShapeDtypeStruct((slab, kw), F32),
            jax.ShapeDtypeStruct((qslab, qw), F32),
            jax.ShapeDtypeStruct((HP, 128), F32),
        ],
        in_specs=[ANY] + [VMEM] * 10 + [SMEM] + [VMEM] * 3,
        out_specs=[VMEM] * 4,
        scratch_shapes=[
            buf(ni, nj, CZ, dtype=BF16),
            buf(F_ALL, ni),
            buf(F_ALL, nj),
            buf(G_ALL, nj),
            buf(G_ALL, ni),
            buf(nj, F_ALL),
            buf(nj, 6 * F_ALL, dtype=BF16),
            buf(6 * F_ALL, lanes, dtype=BF16),
            buf(nj, 3 * G_ALL, dtype=BF16),
            buf(3 * G_ALL, lanes, dtype=BF16),
            buf(2, F_ALL, nj, dtype=BF16),
            buf(2, G_END - G_PT, nj, dtype=BF16),
            buf(128, 128),
            buf(ni, HP, 128),
            buf(nj, lanes),
            buf(nj, lanes),
            buf(256, 1024, dtype=BF16),
            buf(nj, lanes, dtype=BF16),
            buf(nj, lanes, dtype=BF16),
            buf(nj, lanes, dtype=BF16),
            buf(nj, lanes, dtype=BF16),
            buf(nz * ny, 2, slab, kw),
            buf(nx, 2, qslab, qw),
            buf(3, groups, 128),
            buf(nx - 1, 3, groups, 128),
            buf(3, groups, 128),
            buf(3, groups, 128),
            buf(2, groups, 128),
            buf(nz * ny, slab, kw),
            buf(nz, ny, slab, kw),
            buf(ny - 1, nz, slab, kw),
            buf(nz, slab, kw),
            buf(nz - 1, slab, kw),
            buf(nx - 1, 2, qslab, qw),
            buf(2, qslab, qw),
            buf(qslab, qw),
            buf(HP, 128),
            buf(nx, HP, 128),
            buf(HP, 128),
            buf(HP, 128),
            buf(ny, HP, 128),
            buf(nz, HP, 128),
            pltpu.SemaphoreType.DMA((groups,)),
            pltpu.SemaphoreType.DMA((sends,)),
            pltpu.SemaphoreType.DMA((sends,)),
        ],
        compiler_params=pltpu.CompilerParams(
            collective_id=0, has_side_effects=True, vmem_limit_bytes=56 * 2**20
        ),
        name="tile_and_reduce",
    )(pair, bw, hw, q, k, v, qp, kp, vp, rot, tr, count, go, gpt, gpair)

    def whole(a):
        return pl.BlockSpec(a.shape, lambda g, n=len(a.shape): (0,) * n)

    outs = [
        jax.ShapeDtypeStruct((ni, nj, CZ), BF16),
        jax.ShapeDtypeStruct((H * C, qslab), F32),
        jax.ShapeDtypeStruct((3, H * PQ, qslab), F32),
        jax.ShapeDtypeStruct((3, 4, qslab), F32),
        jax.ShapeDtypeStruct((H * C, slab), F32),
        jax.ShapeDtypeStruct((H * C, slab), F32),
        jax.ShapeDtypeStruct((3, H * PQ, slab), F32),
        jax.ShapeDtypeStruct((3, H * PV, slab), F32),
        jax.ShapeDtypeStruct((3, 4, slab), F32),
        jax.ShapeDtypeStruct((CZ, H), F32),
        jax.ShapeDtypeStruct((1, H), F32),
    ]
    small = [bw, hw, kfin, qfin, wfin, qp, kp, vp, rot, tr, gpt]
    res = pl.pallas_call(
        functools.partial(finish, dims),
        grid=(groups,),
        out_shape=outs,
        in_specs=[
            pl.BlockSpec((nj, 256), lambda g: (0, g)),
            pl.BlockSpec((8, H, CZ), lambda g: (g, 0, 0)),
        ]
        + [whole(a) for a in small],
        out_specs=[pl.BlockSpec((8, nj, CZ), lambda g: (g, 0, 0))] + [whole(a) for a in outs[1:]],
        scratch_shapes=[
            buf(8, HP, 128),
            buf(128, 128),
            buf(128, kw),
            buf(128, qw),
            buf(256, 1024, dtype=BF16),
        ],
        name="pair_and_frames",
    )(ab, gpair, *small)
    return (*res[:-1], res[-1].reshape(H))


def solution(mesh):
    finer = Mesh(mesh.devices.reshape(4, 4, 2, 4, 2), ("row_0", "row_1", "row_2", "col_0", "col_1"))
    return sharded(finer, 64, 256)


def sharded(finer, ni, nj):
    sizes = finer.shape
    dims = (sizes["row_0"], sizes["row_1"], sizes["col_0"], ni, nj)
    in_specs = (
        P(ROW, COL, None),
        P(),
        P(),
        P(None, ROW),
        P(None, COL),
        P(None, COL),
        P(None, None, ROW),
        P(None, None, COL),
        P(None, None, COL),
        P(),
        P(),
        P(),
        P(None, ROW),
        P(None, None, ROW),
        P(ROW, None, None),
    )
    out_specs = (
        P(ROW, COL, None),
        P(None, ROW_COL),
        P(None, None, ROW_COL),
        P(None, None, ROW_COL),
        P(None, COL_ROW),
        P(None, COL_ROW),
        P(None, None, COL_ROW),
        P(None, None, COL_ROW),
        P(None, None, COL_ROW),
        P(),
        P(),
    )
    return jax.shard_map(
        functools.partial(per_device, dims),
        mesh=finer,
        in_specs=in_specs,
        out_specs=out_specs,
        check_vma=False,
    )
```

time: 418 us -> 79.7 us (0.19)
  waiting for transfers between devices: 222 us -> 0 us
  Pallas kernels: 0 us -> 58.7 us
  blocking collectives: 48.8 us -> 0 us
  matrix products: 42.1 us -> 0 us
  starting transfers between devices: 31.5 us -> 0 us
  local copies, waits for them, and re-layouts: 45.3 us -> 18.9 us
  between operations: 16.3 us -> 1.31 us
  other arithmetic: 9.25 us -> 0 us
    unnamed x2 -> x0, waiting for transfers between devices: 206 us -> none
    pallas_call x0 -> x2, Pallas kernels: none -> 58.7 us  [the longest x1 49.7 us: per_device(): pl.pallas_call(functools.partial(mega, dims), out_shape=[jax.ShapeDtypeSt...]
    psum x5 -> x0, blocking collectives: 48.8 us -> none  [by_axis(): return functools.reduce(lax.psum, axes, shard)]
    dot_general x27 -> x0, matrix products: 42.1 us -> none  [the longest x1 7.44 us: per_device(): jnp.einsum('hij,ihc->ijc', attn_rounded, grad_pair, preferred_element_typ...]
    all_to_all x4 -> x0, starting transfers between devices: 31.2 us -> none  [the longest x2 20.5 us: from_everyone(): lax.all_to_all(jnp.broadcast_to(shard[None], (count, *shard.shape)), axis...]
    all_to_all x4 -> x0, waiting for transfers between devices: 15.6 us -> none  [the longest x2 9.97 us: from_everyone(): lax.all_to_all(jnp.broadcast_to(shard[None], (count, *shard.shape)), axis...]
    another operation x6 -> x0, local copies, waits for them, and re-layouts: 8.47 us -> none  [split_up(): return jnp.moveaxis(shard.reshape(*before, count, -1, *after), dim, 0)]
    unnamed x96 -> x12, local copies, waits for them, and re-layouts: 11.8 us -> 18.9 us
  transfers between devices with their start and end apart: 5 -> 0, of which waited for: 3 -> 0; matrix products, arithmetic and copies ran while one was open for 11% -> 0% of each run, Pallas kernels for 0% -> 0%
where the time goes in v1:
time: 79.7 us; the launch traced here: 79 us
  Pallas kernels  58.7 us (74%)
  local copies, waits for them, and re-layouts  18.9 us (24%)
  between operations  1.31 us (2%)
    pallas_call x1, Pallas kernels, per_device(): pl.pallas_call(functools.partial(mega, dims), out_shape=[jax.ShapeDtypeSt...  49.7 us
    unnamed x12, local copies, waits for them, and re-layouts  18.9 us
    pallas_call x1, Pallas kernels, per_device(): pl.pallas_call(functools.partial(finish, dims), grid=(groups,), out_shape...  9.05 us

profile of v1, /device:TPU:1, one launch (start us, length us, event | category | flops | bytes accessed | tf_op | source)
XLA Modules:
  0.0 79.0 jit_solution(5143171105841113029)
XLA Ops:
  1.3 1.4 %copy.26.bw_ref = bf16[128,12]{1,0:T(8,128)(2,1)} copy(bf16[128,12]{0,1:T(8,128)(2,1)} %param.16) | data formatting | bytes 6144 | tf_op args[1]
  2.7 1.6 %copy.27.q_ref = f32[192,64]{1,0:T(8,128)} copy(f32[192,64]{0,1:T(8,128)} %param.18) | data formatting | bytes 98304 | tf_op args[3]
  4.3 1.6 %copy.28.go_ref = f32[192,64]{1,0:T(8,128)} copy(f32[192,64]{0,1:T(8,128)} %param.27) | data formatting | bytes 98304 | tf_op args[12]
  5.8 1.7 %copy.29.gpt_ref = f32[3,96,64]{2,1,0:T(8,128)} copy(f32[3,96,64]{1,2,0:T(8,128)} %param.28) | data formatting | bytes 147456 | tf_op args[13]
  7.5 1.8 %copy.30.gpair_ref = bf16[64,12,128]{2,1,0:T(8,128)(2,1)} copy(bf16[64,12,128]{2,0,1:T(8,128)(2,1)} %param.29) | data formatting | bytes 393216 | tf_op args[14]
  9.3 49.7 %tile_and_reduce.1 = (bf16[256,2048]{1,0:T(8,128)(2,1)}, f32[8,896]{1,0:T(8,128)}, f32[8,768]{1,0:T(8,128)}, f32[16,128]{1,0:T(8,128)}) custom-call(bf16[64,256,128]{2,1,0:T(8,128)(2,1)} %pair_hbm.1, bf16[128,12]{1,0:T(8,128)(2,1)} %copy.26.bw_ref, f32[1,12]{1,0:T(1,128)} %bitcast.2, f32[192,64]{1,0:T(8,128)} %copy.27.q_ref, f32[192,256]{1,0:T(8,128)} %k_ref.1, ...), custom_call_target="tpu_custom_call" | custom-call | tf_op jit(solution)/shard_map/tile_and_reduce/pallas_call | solution.py:651
  59.0 9.0 %pair_and_frames.1 = (bf16[64,256,128]{2,1,0:T(8,128)(2,1)}, f32[192,8]{1,0:T(8,128)}, f32[3,48,8]{2,1,0:T(8,128)}, f32[3,4,8]{2,1,0:T(4,128)}, f32[192,8]{1,0:T...) custom-call(bf16[256,2048]{1,0:T(8,128)(2,1)} %get-tuple-element.26., ...), custom_call_target="tpu_custom_call" | custom-call | tf_op jit(solution)/shard_map/pair_and_frames/pallas_call | solution.py:731
  68.0 1.6 %copy.34 = f32[192,8]{0,1:T(8,128)} copy(f32[192,8]{1,0:T(8,128)} %get-tuple-element.42) | data formatting | bytes 12288
  69.6 1.6 %copy.36 = f32[192,8]{0,1:T(8,128)} copy(f32[192,8]{1,0:T(8,128)} %get-tuple-element.45) | data formatting | bytes 12288
  71.2 1.6 %copy.37 = f32[192,8]{0,1:T(8,128)} copy(f32[192,8]{1,0:T(8,128)} %get-tuple-element.46) | data formatting | bytes 12288
  72.7 1.5 %copy.40 = f32[128,12]{0,1:T(8,128)} copy(f32[128,12]{1,0:T(8,128)} %get-tuple-element.50) | data formatting | bytes 12288
  74.2 1.6 %copy.35 = f32[3,48,8]{1,2,0:T(8,128)} copy(f32[3,48,8]{2,1,0:T(8,128)} %get-tuple-element.43) | data formatting | bytes 9216
  75.8 1.6 %copy.38 = f32[3,48,8]{1,2,0:T(8,128)} copy(f32[3,48,8]{2,1,0:T(8,128)} %get-tuple-element.47) | data formatting | bytes 9216
  77.4 1.6 %copy.39 = f32[3,96,8]{1,2,0:T(8,128)} copy(f32[3,96,8]{2,1,0:T(8,128)} %get-tuple-element.48) | data formatting | bytes 18432

commit v2 on v1

--- a/solution.py
+++ b/solution.py
@@ -150,18 +150,24 @@
     dl_s,
     ah_s,
     al_s,
-    kout_s,
     qout_s,
     st_s,
     xst_s,
     cst_s,
     zst_s,
     sc_s,
-    kc_s,
-    ksum_s,
-    ky_s,
-    kz_s,
-    kr_s,
+    s0_s,
+    sc0_s,
+    s1_s,
+    sz_s,
+    s2_s,
+    sr_s,
+    v0_s,
+    vc0_s,
+    v1_s,
+    vy_s,
+    v2_s,
+    vr_s,
     qx_s,
     qz_s,
     qr_s,
@@ -233,8 +239,8 @@
 
     norm_sel = ((iota((HP, 48), 1) >> 2) == iota((HP, 48), 0)).astype(F32)
     qg = rotate(rot_q, [qp_ref[b] for b in range(3)], tr_q)
-    gg = rotate(rot_q, [gpt_ref[b] for b in range(3)])
-    qf_s[0:F_PT] = q_ref[...]
+    gg = rotate(rot_q, [jnp.transpose(gpt_ref[b]) for b in range(3)])
+    qf_s[0:F_PT] = jnp.transpose(q_ref[...])
     for a in range(3):
         qf_s[F_PT + 48 * a : F_PT + 48 * (a + 1)] = qg[a]
     qf_s[F_N1:F_N2] = jnp.ones((HP, ni), F32)
@@ -242,7 +248,7 @@
         norm_sel, qg[0] * qg[0] + qg[1] * qg[1] + qg[2] * qg[2], precision=HIGHEST
     )
     qf_s[F_N2 + HP :] = jnp.zeros((F_ALL - F_N2 - HP, ni), F32)
-    gf_s[0:G_PT] = go_ref[...]
+    gf_s[0:G_PT] = jnp.transpose(go_ref[...])
     for a in range(3):
         gf_s[G_PT + 96 * a : G_PT + 96 * (a + 1)] = gg[a]
     gf_s[G_END:] = jnp.zeros((G_ALL - G_END, ni), F32)
@@ -306,12 +312,12 @@
 
     lax.fori_loop(0, chunks, expand, 0)
 
-    w_s[...] = jnp.zeros((128, 128), F32)
-    w_s[:, 0:H] = bw_ref[...].astype(F32)
-    wt = jnp.transpose(w_s[...])[0:HP]
-    g_s[...] = jnp.zeros((ni, HP, 128), F32)
-    g_s[:, 0:H, :] = gpair_ref[...].astype(F32)
-    w_rows = jnp.concatenate([wt] * 8, axis=0)
+    w_s[...] = jnp.zeros((HP, 128), F32)
+    w_s[0:H] = bw_ref[...].astype(F32)
+    g_s[...] = jnp.zeros((lanes, 128), F32)
+    for b in range(H):
+        g_s[pl.ds(b, ni, stride=HP), :] = gpair_ref[b].astype(F32)
+    w_rows = jnp.concatenate([w_s[...]] * 8, axis=0)
     for b in range(8):
         rhs_s[0:128, 128 * b : 128 * (b + 1)] = pair_rows(w_rows, b)
 
@@ -326,7 +332,7 @@
             pltpu.make_async_copy(
                 pair_hbm.at[pl.ds(8 * g, 8)], pair_v.at[pl.ds(8 * g, 8)], pair_sem.at[g]
             ).wait()
-            g_rows = g_s[pl.ds(8 * g, 8)].reshape(128, 128)
+            g_rows = g_s[tile(g, 128)]
             for b in range(8):
                 rhs_s[128:256, 128 * b : 128 * (b + 1)] = pair_rows(g_rows, b)
             acc = None
@@ -387,40 +393,63 @@
         scaled = WL * dlog
         ab_out[:, pl.ds(pl.multiple_of(g * 256, 256), 128)] = scaled.astype(BF16)
         ab_out[:, pl.ds(pl.multiple_of(g * 256 + 128, 128), 128)] = a_hi
-        turned = jnp.transpose(scaled).astype(BF16)
+        turned = jnp.transpose(dlog).astype(BF16)
         for b in range(8):
             acc = acc + mm(turned[16 * b : 16 * (b + 1)], pair_v[8 * g + b])
         return acc
 
     weight = lax.fori_loop(0, groups, weights_of, jnp.zeros((HP, 128), F32))
 
+    slab = nj // (nz * ny * 2)
+
+    def add(terms):
+        return functools.reduce(lambda a, b: a + b, terms)
+
+    def spread_to(src, dst, axis, me, count, slot):
+        out = []
+        for r in range(1, count):
+            peer = lax.rem(me + r, count)
+            out.append(send(src.at[slot(peer)], dst.at[r - 1], {axis: peer}))
+        return out
+
+    def done(copies):
+        for copy in copies:
+            copy.wait()
+
     kout = mm_nt(dh_s[...], qcat_s[0:F_ALL])
     kout += mm_nt(dh_s[...], qcat_s[F_ALL : 2 * F_ALL])
     kout += mm_nt(dl_s[...], qcat_s[0:F_ALL])
+    s0_s[...] = kout.reshape(s0_s.shape)
+    s_core = send(s0_s.at[:, :, 1 - c], sc0_s, {"row_2": 1 - c})
+    spread = jnp.sum(kt_s[...] * kout, axis=0, keepdims=True)
+
+    wm_s[0:H] = WL * weight[0:H]
+    wm_s[H : H + 1] = spread[:, 128:256]
+    wm_s[H + 1 : H + 2] = spread[:, 256:384]
+    wm_s[H + 2 :] = jnp.zeros((HP - H - 2, 128), F32)
+
+    def share(src, slots, axis, me, count):
+        slots[me] = src[...]
+        return [send(src, slots.at[me], {axis: lax.rem(me + r, count)}) for r in range(1, count)]
+
+    def settle(copies, slots, dst, count):
+        done(copies)
+        dst[...] = add([slots[n] for n in range(count)])
+
+    w_x = share(wm_s, wx_s, "col_0", x, nx)
+
     aout = mm_nt(ah_s[...], gcat_s[0:G_ALL])
     aout += mm_nt(ah_s[...], gcat_s[G_ALL : 2 * G_ALL])
     aout += mm_nt(al_s[...], gcat_s[0:G_ALL])
-    slab = nj // (nz * ny * 2)
-    kout_s[:, :, :, 0:F_ALL] = kout.reshape(nz * ny, 2, slab, F_ALL)
-    kout_s[:, :, :, F_ALL:] = aout.reshape(nz * ny, 2, slab, G_ALL)
-    core_copy = send(kout_s.at[:, 1 - c], kc_s, {"row_2": 1 - c})
-    spread = jnp.sum(kt_s[...] * kout, axis=0, keepdims=True)
-
-    wm_s[0:H] = weight[0:H]
-    wm_s[H : H + 1] = spread[:, 128:256]
-    wm_s[H + 1 : H + 2] = spread[:, 256:384]
-    wm_s[H + 2 :] = jnp.zeros((HP - H - 2, 128), F32)
-
-    def share(src, slots, axis, me, count):
-        slots[me] = src[...]
-        return [send(src, slots.at[me], {axis: lax.rem(me + r, count)}) for r in range(1, count)]
-
-    def settle(copies, slots, dst, count):
-        for copy in copies:
-            copy.wait()
-        dst[...] = functools.reduce(lambda a, b: a + b, [slots[n] for n in range(count)])
-
-    wx_copies = share(wm_s, wx_s, "col_0", x, nx)
+    v0_s[...] = aout.reshape(v0_s.shape)
+    v_core = send(v0_s.at[:, :, 1 - c], vc0_s, {"row_2": 1 - c})
+
+    s_core.wait()
+    s1_s[...] = s0_s[:, :, c] + sc0_s[...]
+    s_z = spread_to(s1_s, sz_s, "row_0", z, nz, lambda p: p)
+    v_core.wait()
+    v1_s[...] = v0_s[:, :, c] + vc0_s[...]
+    v_y = spread_to(v1_s, vy_s, "row_1", y, ny, lambda p: (slice(None), p))
 
     def query_side(n, acc):
         at = tile(n, 256)
@@ -438,59 +467,43 @@
             outs.append(mm_nt(e, hi) + mm_nt(e, lo))
         return acc[0] + outs[0], acc[1] + outs[1]
 
-    q1, q2 = lax.fori_loop(
-        0,
-        chunks,
-        query_side,
-        (jnp.zeros((ni, F_ALL), F32), jnp.zeros((ni, G_END - G_PT), F32)),
-    )
+    sums = (jnp.zeros((ni, F_ALL), F32), jnp.zeros((ni, G_END - G_PT), F32))
+    sums = lax.fori_loop(0, chunks // 2, query_side, sums)
+    settle(w_x, wx_s, wm_s, nx)
+    w_w = send(wm_s, wz_s, {"col_1": 1 - w})
+    q1, q2 = lax.fori_loop(chunks // 2, chunks, query_side, sums)
     qslab = ni // (nx * 2)
     qout_s[:, :, :, 0:F_ALL] = q1.reshape(nx, 2, qslab, F_ALL)
     qout_s[:, :, :, F_ALL : F_ALL + G_END - G_PT] = q2.reshape(nx, 2, qslab, G_END - G_PT)
     qout_s[:, :, :, F_ALL + G_END - G_PT :] = jnp.zeros(
         (nx, 2, qslab, qout_s.shape[3] - F_ALL - G_END + G_PT), F32
     )
-    qx_copies = []
-    for r in range(1, nx):
-        peer = lax.rem(x + r, nx)
-        qx_copies.append(send(qout_s.at[peer], qx_s.at[r - 1], {"col_0": peer}))
-
-    core_copy.wait()
-    ksum_s[...] = (kout_s[:, c] + kc_s[...]).reshape(ksum_s.shape)
-    ky_copies = []
-    for r in range(1, ny):
-        peer = lax.rem(y + r, ny)
-        ky_copies.append(send(ksum_s.at[:, peer], ky_s.at[r - 1], {"row_1": peer}))
-
-    settle(wx_copies, wx_s, wm_s, nx)
-    wz_copy = send(wm_s, wz_s, {"col_1": 1 - w})
-    for copy in qx_copies:
-        copy.wait()
-    qz_s[...] = functools.reduce(lambda a, b: a + b, [qx_s[r] for r in range(nx - 1)], qout_s[x])
-    qz_copy = send(qz_s.at[1 - w], qr_s, {"col_1": 1 - w})
-
-    for copy in ky_copies:
-        copy.wait()
-    kz_s[...] = functools.reduce(lambda a, b: a + b, [ky_s[r] for r in range(ny - 1)], ksum_s[:, y])
-    kz_copies = []
-    for r in range(1, nz):
-        peer = lax.rem(z + r, nz)
-        kz_copies.append(send(kz_s.at[peer], kr_s.at[r - 1], {"row_0": peer}))
-
-    wz_copy.wait()
+    q_x = spread_to(qout_s, qx_s, "col_0", x, nx, lambda p: p)
+
+    done(s_z)
+    s2_s[...] = add([s1_s[z]] + [sz_s[r] for r in range(nz - 1)])
+    s_y = spread_to(s2_s, sr_s, "row_1", y, ny, lambda p: p)
+    w_w.wait()
     wm_s[...] = wm_s[...] + wz_s[...]
-    wc_copy = send(wm_s, wc_s, {"row_2": 1 - c})
-    wc_copy.wait()
+    w_c = send(wm_s, wc_s, {"row_2": 1 - c})
+    done(v_y)
+    v2_s[...] = add([v1_s[:, y]] + [vy_s[r] for r in range(ny - 1)])
+    v_z = spread_to(v2_s, vr_s, "row_0", z, nz, lambda p: p)
+    w_c.wait()
     wm_s[...] = wm_s[...] + wc_s[...]
-    wy_copies = share(wm_s, wy_s, "row_1", y, ny)
-    qz_copy.wait()
+    w_y = share(wm_s, wy_s, "row_1", y, ny)
+    done(q_x)
+    qz_s[...] = add([qout_s[x]] + [qx_s[r] for r in range(nx - 1)])
+    q_w = send(qz_s.at[1 - w], qr_s, {"col_1": 1 - w})
+    settle(w_y, wy_s, wm_s, ny)
+    w_z = share(wm_s, wr_s, "row_0", z, nz)
+    done(s_y)
+    kfin_ref[:, 0:F_ALL] = add([s2_s[y]] + [sr_s[r] for r in range(ny - 1)])
+    done(v_z)
+    kfin_ref[:, F_ALL:] = add([v2_s[z]] + [vr_s[r] for r in range(nz - 1)])
+    q_w.wait()
     qfin_ref[...] = qz_s[w] + qr_s[...]
-    settle(wy_copies, wy_s, wm_s, ny)
-    wr_copies = share(wm_s, wr_s, "row_0", z, nz)
-    for copy in kz_copies:
-        copy.wait()
-    kfin_ref[...] = functools.reduce(lambda a, b: a + b, [kr_s[r] for r in range(nz - 1)], kz_s[z])
-    settle(wr_copies, wr_s, wfin_ref, nz)
+    settle(w_z, wr_s, wfin_ref, nz)
 
 
 def finish(
@@ -522,8 +535,9 @@
     g_s,
     w_s,
     t_s,
-    tq_s,
     rhs_s,
+    pair_v,
+    pair_sem,
 ):
     nz, ny, nx, ni, nj = dims
     z, y, c = lax.axis_index("row_0"), lax.axis_index("row_1"), lax.axis_index("row_2")
@@ -533,117 +547,152 @@
     slab = nj // (nz * ny * 2)
     qslab = ni // (nx * 2)
 
-    @pl.when(pl.program_id(0) == 0)
-    def _():
-        w_s[...] = jnp.zeros((128, 128), F32)
-        w_s[:, 0:H] = bw_ref[...].astype(F32)
-        w_rows = jnp.concatenate([jnp.transpose(w_s[...])[0:HP]] * 8, axis=0)
+    w_s[...] = jnp.zeros((HP, 128), F32)
+    w_s[0:H] = bw_ref[...].astype(F32)
+    w_rows = jnp.concatenate([w_s[...]] * 8, axis=0)
+    for b in range(8):
+        rhs_s[0:128, 128 * b : 128 * (b + 1)] = pair_rows(w_rows, b)
+    g_s[...] = jnp.zeros(g_s.shape, F32)
+    for b in range(H):
+        g_s[pl.ds(b, ni, stride=HP), :] = gpair_ref[b].astype(F32)
+
+    def copy_out(g):
+        at = pl.ds(pl.multiple_of(8 * g, 8), 8)
+        return pltpu.make_async_copy(pair_v.at[at], pair_out.at[at], pair_sem.at[g])
+
+    groups = ni // 8
+
+    def pair_group(g, _):
+        g_rows = g_s[tile(g, 128)]
         for b in range(8):
-            rhs_s[0:128, 128 * b : 128 * (b + 1)] = pair_rows(w_rows, b)
-        g_s[...] = jnp.zeros(g_s.shape, F32)
-
-    g_s[:, 0:H, :] = gpair_ref[...].astype(F32)
-    g_rows = g_s[...].reshape(128, 128)
-    for b in range(8):
-        rhs_s[128:256, 128 * b : 128 * (b + 1)] = pair_rows(g_rows, b)
-    for b in range(4):
-        two = mm(ab_ref[...], rhs_s[:, 256 * b : 256 * (b + 1)]).astype(BF16)
-        pair_out[2 * b] = two[:, :128]
-        pair_out[2 * b + 1] = two[:, 128:]
-
-    @pl.when(pl.program_id(0) == 0)
-    def _():
-        def pick(count, start):
-            return (iota((count, 128), 0) == start + iota((count, 128), 1)).astype(F32)
-
-        def exact(a, b):
-            return jnp.dot(a, b, precision=HIGHEST)
-
-        def split_rows(t):
-            return [t[b : b + 1] for b in range(3)]
-
-        expand = ((iota((48, HP), 0) >> 2) == iota((48, HP), 1)).astype(F32)
-        coef = coef_column(hw_ref, iota((48, 1), 0) >> 2)
-
-        at = row * slab
-        sel = pick(128, lax.rem(at, 128))
-        base = tile(col * (nj // 128) + at // 128, 128)
-        here = tile(at // 128, 128)
-        rot = [split_rows(exact(rot_ref[a, :, base], sel)) for a in range(3)]
-        shift = split_rows(exact(tr_ref[:, base], sel))
-        kp = [exact(kp_ref[b, :, here], sel) for b in range(3)]
-        vp = [exact(vp_ref[b, :, here], sel) for b in range(3)]
-        kg = rotate(rot, kp, shift)
-        t_s[...] = jnp.zeros(t_s.shape, F32)
-        t_s[0:slab] = kfin_ref[...]
-        kt = jnp.transpose(t_s[...])
-        k_out[...] = (WL * WS) * kt[0:F_PT, :slab]
-        v_out[...] = kt[F_ALL : F_ALL + G_PT, :slab]
-        sums = exact(expand, kt[F_N1:F_N2])
-        dkg = [
-            2.0 * coef * (kt[F_PT + 48 * a : F_PT + 48 * (a + 1)] - kg[a] * sums) for a in range(3)
-        ]
-        v_at = F_ALL + G_PT
-        dvg = [kt[v_at + 96 * a : v_at + 96 * (a + 1)] for a in range(3)]
-        for b in range(3):
-            kp_out[b] = (rot[0][b] * dkg[0] + rot[1][b] * dkg[1] + rot[2][b] * dkg[2])[:, :slab]
-            vp_out[b] = (rot[0][b] * dvg[0] + rot[1][b] * dvg[1] + rot[2][b] * dvg[2])[:, :slab]
-
-        def over(t):
-            return jnp.sum(t, axis=0, keepdims=True)
-
+            rhs_s[128:256, 128 * b : 128 * (b + 1)] = pair_rows(g_rows, b)
+        for b in range(4):
+            two = mm(ab_ref[:, tile(g, 256)], rhs_s[:, 256 * b : 256 * (b + 1)]).astype(BF16)
+            pair_v[8 * g + 2 * b] = two[:, :128]
+            pair_v[8 * g + 2 * b + 1] = two[:, 128:]
+        copy_out(g).start()
+        return 0
+
+    lax.fori_loop(0, groups, pair_group, 0)
+
+    def exact(a, b):
+        return jnp.dot(a, b, precision=HIGHEST)
+
+    def from_lane(rows, at):
+        return pltpu.roll(rows, lax.rem(128 - at, 128), 1)
+
+    def over(t):
+        return jnp.sum(t, axis=1, keepdims=True)
+
+    def columns(t):
+        return [[t[:, 3 * a + b : 3 * a + b + 1] for b in range(3)] for a in range(3)]
+
+    def back(rot, v):
+        return [rot[0][b] * v[0] + rot[1][b] * v[1] + rot[2][b] * v[2] for b in range(3)]
+
+    def frame(out, cols, count):
+        t = jnp.zeros((count, 128), F32)
+        for n in range(12):
+            t = jnp.where(iota((count, 128), 1) == n, cols[n // 4][n % 4], t)
+        t_s[0:count] = t
+        turned = jnp.transpose(t_s[0:128])
         for a in range(3):
-            for b in range(3):
-                kf_out[a, b : b + 1] = (over(dkg[a] * kp[b]) + over(dvg[a] * vp[b]))[:, :slab]
-            kf_out[a, 3:4] = (over(dkg[a]) + over(dvg[a]))[:, :slab]
-
-        inner = c * ni + col * qslab
-        sel = pick(128, inner)
-        base = tile(z * ny + y, 128)
-        rot = [split_rows(exact(rot_ref[a, :, base], sel)) for a in range(3)]
-        shift = split_rows(exact(tr_ref[:, base], sel))
-        sel = pick(ni, col * qslab)
-        qp = [exact(qp_ref[b], sel) for b in range(3)]
-        gp = [exact(gpt_ref[b], sel) for b in range(3)]
-        qg = rotate(rot, qp, shift)
-        gg = rotate(rot, gp)
-        tq_s[...] = jnp.zeros(tq_s.shape, F32)
-        tq_s[0:qslab] = qfin_ref[...]
-        qt = jnp.transpose(tq_s[...])
-        q_out[...] = (WL * WS) * qt[0:F_PT, :qslab]
-        sums = exact(expand, qt[F_N2 : F_N2 + HP])
-        dqg = [
-            -2.0 * coef * (qg[a] * sums - qt[F_PT + 48 * a : F_PT + 48 * (a + 1)]) for a in range(3)
-        ]
-        opt = [qt[F_ALL + 96 * a : F_ALL + 96 * (a + 1)] - shift[a] for a in range(3)]
-        for b in range(3):
-            qp_out[b] = (rot[0][b] * dqg[0] + rot[1][b] * dqg[1] + rot[2][b] * dqg[2])[:, :qslab]
-        for a in range(3):
-            for b in range(3):
-                qf_out[a, b : b + 1] = (over(dqg[a] * qp[b]) + over(opt[a] * gp[b]))[:, :qslab]
-            qf_out[a, 3:4] = (over(dqg[a]) - over(gg[a]))[:, :qslab]
-
-        w_s[...] = jnp.zeros((128, 128), F32)
-        w_s[0:HP] = wfin_ref[...]
-        w_out[...] = jnp.transpose(w_s[...])[:, 0:H]
-        total = jnp.zeros((1, 128), F32)
-        for n in range(2):
-            f = iota((128, 128), 0) + 128 * (n + 1)
-            keep = (head_of_feature(f) == iota((128, 128), 1)) & (f >= F_PT)
-            total += exact(wfin_ref[H + n : H + n + 1], keep.astype(F32))
-        hw = hw_ref[...]
-        hw_out[...] = total[:, 0:H] / (softplus(hw) * (1.0 + jnp.exp(-hw)))
+            out[a] = turned[4 * a : 4 * a + 4, :count]
+
+    expand = (iota((HP, 48), 0) == (iota((HP, 48), 1) >> 2)).astype(F32)
+    coef = jnp.broadcast_to(coef_column(hw_ref, iota((48, 1), 0) >> 2), (48, 48))
+    coef = jnp.where(iota((48, 48), 0) == iota((48, 48), 1), coef, 0.0)
+    coef = jnp.sum(coef, axis=0, keepdims=True)
+
+    t_s[...] = jnp.zeros(t_s.shape, F32)
+    at = row * slab
+    base = tile(col * (nj // 128) + at // 128, 128)
+    here = tile(at // 128, 128)
+    for a in range(3):
+        t_s[3 * a : 3 * a + 3] = rot_ref[a, :, base]
+        t_s[16 + 48 * a : 16 + 48 * (a + 1)] = kp_ref[a, :, here]
+        t_s[160 + 96 * a : 160 + 96 * (a + 1)] = vp_ref[a, :, here]
+    t_s[9:12] = tr_ref[:, base]
+    own = jnp.transpose(from_lane(t_s[...], lax.rem(at, 128)))[:slab]
+    rot = columns(own)
+    shift = [own[:, 9 + a : 10 + a] for a in range(3)]
+    kp = [own[:, 16 + 48 * b : 16 + 48 * (b + 1)] for b in range(3)]
+    vp = [own[:, 160 + 96 * b : 160 + 96 * (b + 1)] for b in range(3)]
+    kg = rotate(rot, kp, shift)
+    k_out[...] = (WL * WS) * kfin_ref[:, 0:F_PT]
+    v_out[...] = kfin_ref[:, F_ALL : F_ALL + G_PT]
+    sums = exact(kfin_ref[:, F_N1:F_N2], expand)
+    dkg = []
+    for a in range(3):
+        part = kfin_ref[:, F_PT + 48 * a : F_PT + 48 * (a + 1)]
+        dkg.append(2.0 * coef * (part - kg[a] * sums))
+    v_at = F_ALL + G_PT
+    dvg = [kfin_ref[:, v_at + 96 * a : v_at + 96 * (a + 1)] for a in range(3)]
+    for b, (dk, dv) in enumerate(zip(back(rot, dkg), back(rot, dvg))):
+        kp_out[b] = dk
+        vp_out[b] = dv
+    cols = []
+    for a in range(3):
+        cols.append([over(dkg[a] * kp[b]) + over(dvg[a] * vp[b]) for b in range(3)])
+        cols[a].append(over(dkg[a]) + over(dvg[a]))
+    frame(kf_out, cols, slab)
+
+    at = col * qslab
+    base = tile(z * ny + y, 128)
+    t_s[...] = jnp.zeros(t_s.shape, F32)
+    for a in range(3):
+        t_s[3 * a : 3 * a + 3] = rot_ref[a, :, base]
+        t_s[16 + 48 * a : 16 + 48 * (a + 1), 0:ni] = qp_ref[a]
+    t_s[9:12] = tr_ref[:, base]
+    t_s[0:16] = from_lane(t_s[0:16], c * ni + at)
+    t_s[16:160] = from_lane(t_s[16:160], at)
+    own = jnp.transpose(t_s[0:256])[:qslab]
+    rot = columns(own)
+    shift = [own[:, 9 + a : 10 + a] for a in range(3)]
+    qp = [own[:, 16 + 48 * b : 16 + 48 * (b + 1)] for b in range(3)]
+    gp = [gpt_ref[b, tile(col, qslab), :] for b in range(3)]
+    qg = rotate(rot, qp, shift)
+    gg = rotate(rot, gp)
+    q_out[...] = (WL * WS) * qfin_ref[:, 0:F_PT]
+    sums = exact(qfin_ref[:, F_N2 : F_N2 + HP], expand)
+    dqg = []
+    for a in range(3):
+        part = qfin_ref[:, F_PT + 48 * a : F_PT + 48 * (a + 1)]
+        dqg.append(-2.0 * coef * (qg[a] * sums - part))
+    opt = [qfin_ref[:, F_ALL + 96 * a : F_ALL + 96 * (a + 1)] - shift[a] for a in range(3)]
+    for b, dq in enumerate(back(rot, dqg)):
+        qp_out[b] = dq
+    cols = []
+    for a in range(3):
+        cols.append([over(dqg[a] * qp[b]) + over(opt[a] * gp[b]) for b in range(3)])
+        cols[a].append(over(dqg[a]) - over(gg[a]))
+    frame(qf_out, cols, qslab)
+
+    w_out[...] = wfin_ref[0:H]
+    total = jnp.zeros((1, 128), F32)
+    for n in range(2):
+        f = iota((128, 128), 0) + 128 * (n + 1)
+        keep = (head_of_feature(f) == iota((128, 128), 1)) & (f >= F_PT)
+        total += exact(wfin_ref[H + n : H + n + 1], keep.astype(F32))
+    hw = hw_ref[...]
+    hw_out[...] = total[:, 0:H] / (softplus(hw) * (1.0 + jnp.exp(-hw)))
+
+    for g in range(groups):
+        copy_out(g).wait()
 
 
 def per_device(dims, *args):
     (pair, bw, hw, q, k, v, qp, kp, vp, rot, tr, count, go, gpt, gpair) = args
     nz, ny, nx, ni, nj = dims
     hw = hw.reshape(1, H)
+    bw, q, go = bw.T, q.T, go.T
+    gpt = jnp.transpose(gpt, (0, 2, 1))
+    gpair = jnp.transpose(gpair, (1, 0, 2))
     lanes = ni * HP
     slab, qslab = nj // (nz * ny * 2), ni // (nx * 2)
     kw, qw = F_ALL + G_ALL, 768
     groups = lanes // 128
-    sends = 2 * ((nx - 1) + 1) + 1 + (ny - 1) + (nz - 1) + (nx - 1) + 1 + 1 + (ny - 1) + (nz - 1)
+    sends = 3 * nx + 3 * (ny - 1) + 3 * (nz - 1) + 3
 
     def buf(*shape, dtype=F32):
         return pltpu.VMEM(shape, dtype)
@@ -671,8 +720,8 @@
             buf(3 * G_ALL, lanes, dtype=BF16),
             buf(2, F_ALL, nj, dtype=BF16),
             buf(2, G_END - G_PT, nj, dtype=BF16),
-            buf(128, 128),
-            buf(ni, HP, 128),
+            buf(HP, 128),
+            buf(lanes, 128),
             buf(nj, lanes),
             buf(nj, lanes),
             buf(256, 1024, dtype=BF16),
@@ -680,18 +729,24 @@
             buf(nj, lanes, dtype=BF16),
             buf(nj, lanes, dtype=BF16),
             buf(nj, lanes, dtype=BF16),
-            buf(nz * ny, 2, slab, kw),
             buf(nx, 2, qslab, qw),
             buf(3, groups, 128),
             buf(nx - 1, 3, groups, 128),
             buf(3, groups, 128),
             buf(3, groups, 128),
             buf(2, groups, 128),
-            buf(nz * ny, slab, kw),
-            buf(nz, ny, slab, kw),
-            buf(ny - 1, nz, slab, kw),
-            buf(nz, slab, kw),
-            buf(nz - 1, slab, kw),
+            buf(nz, ny, 2, slab, F_ALL),
+            buf(nz, ny, slab, F_ALL),
+            buf(nz, ny, slab, F_ALL),
+            buf(nz - 1, ny, slab, F_ALL),
+            buf(ny, slab, F_ALL),
+            buf(ny - 1, slab, F_ALL),
+            buf(nz, ny, 2, slab, G_ALL),
+            buf(nz, ny, slab, G_ALL),
+            buf(nz, ny, slab, G_ALL),
+            buf(ny - 1, nz, slab, G_ALL),
+            buf(nz, slab, G_ALL),
+            buf(nz - 1, slab, G_ALL),
             buf(nx - 1, 2, qslab, qw),
             buf(2, qslab, qw),
             buf(qslab, qw),
@@ -706,48 +761,44 @@
             pltpu.SemaphoreType.DMA((sends,)),
         ],
         compiler_params=pltpu.CompilerParams(
-            collective_id=0, has_side_effects=True, vmem_limit_bytes=56 * 2**20
+            collective_id=0, has_side_effects=True, vmem_limit_bytes=60 * 2**20
         ),
         name="tile_and_reduce",
     )(pair, bw, hw, q, k, v, qp, kp, vp, rot, tr, count, go, gpt, gpair)
 
-    def whole(a):
-        return pl.BlockSpec(a.shape, lambda g, n=len(a.shape): (0,) * n)
-
     outs = [
         jax.ShapeDtypeStruct((ni, nj, CZ), BF16),
-        jax.ShapeDtypeStruct((H * C, qslab), F32),
-        jax.ShapeDtypeStruct((3, H * PQ, qslab), F32),
+        jax.ShapeDtypeStruct((qslab, H * C), F32),
+        jax.ShapeDtypeStruct((3, qslab, H * PQ), F32),
         jax.ShapeDtypeStruct((3, 4, qslab), F32),
-        jax.ShapeDtypeStruct((H * C, slab), F32),
-        jax.ShapeDtypeStruct((H * C, slab), F32),
-        jax.ShapeDtypeStruct((3, H * PQ, slab), F32),
-        jax.ShapeDtypeStruct((3, H * PV, slab), F32),
+        jax.ShapeDtypeStruct((slab, H * C), F32),
+        jax.ShapeDtypeStruct((slab, H * C), F32),
+        jax.ShapeDtypeStruct((3, slab, H * PQ), F32),
+        jax.ShapeDtypeStruct((3, slab, H * PV), F32),
         jax.ShapeDtypeStruct((3, 4, slab), F32),
-        jax.ShapeDtypeStruct((CZ, H), F32),
+        jax.ShapeDtypeStruct((H, CZ), F32),
         jax.ShapeDtypeStruct((1, H), F32),
     ]
     small = [bw, hw, kfin, qfin, wfin, qp, kp, vp, rot, tr, gpt]
     res = pl.pallas_call(
         functools.partial(finish, dims),
-        grid=(groups,),
         out_shape=outs,
-        in_specs=[
-            pl.BlockSpec((nj, 256), lambda g: (0, g)),
-            pl.BlockSpec((8, H, CZ), lambda g: (g, 0, 0)),
-        ]
-        + [whole(a) for a in small],
-        out_specs=[pl.BlockSpec((8, nj, CZ), lambda g: (g, 0, 0))] + [whole(a) for a in outs[1:]],
+        in_specs=[VMEM] * 13,
+        out_specs=[ANY] + [VMEM] * 10,
         scratch_shapes=[
-            buf(8, HP, 128),
-            buf(128, 128),
-            buf(128, kw),
-            buf(128, qw),
+            buf(lanes, 128),
+            buf(HP, 128),
+            buf(512, 128),
             buf(256, 1024, dtype=BF16),
+            buf(ni, nj, CZ, dtype=BF16),
+            pltpu.SemaphoreType.DMA((groups,)),
         ],
+        compiler_params=pltpu.CompilerParams(vmem_limit_bytes=60 * 2**20),
         name="pair_and_frames",
     )(ab, gpair, *small)
-    return (*res[:-1], res[-1].reshape(H))
+    pair_grad, dq, dqp, dqf, dk, dv, dkp, dvp, dkf, dw, dhw = res
+    turn = functools.partial(jnp.transpose, axes=(0, 2, 1))
+    return pair_grad, dq.T, turn(dqp), dqf, dk.T, dv.T, turn(dkp), turn(dvp), dkf, dw.T, dhw[0]
 
 
 def solution(mesh):

time: 79.7 us -> 56 us (0.70)
  local copies, waits for them, and re-layouts: 18.9 us -> 0 us
  Pallas kernels: 58.7 us -> 54.6 us
    unnamed x12 -> x0, local copies, waits for them, and re-layouts: 18.9 us -> none
    pallas_call x1, Pallas kernels: 49.7 us -> 47.4 us  [per_device(): pl.pallas_call(functools.partial(mega, dims), out_shape=[jax.ShapeDtypeSt...]
    pallas_call x1, Pallas kernels: 9.05 us -> 7.12 us  [per_device(): pl.pallas_call(functools.partial(finish, dims), out_shape=outs, in_specs=...]
where the time goes in v2:
time: 56 us; the launch traced here: 55.9 us
  Pallas kernels  54.6 us (98%)
  between operations  1.3 us (2%)
    pallas_call x1, Pallas kernels, per_device(): pl.pallas_call(functools.partial(mega, dims), out_shape=[jax.ShapeDtypeSt...  47.4 us
    pallas_call x1, Pallas kernels, per_device(): pl.pallas_call(functools.partial(finish, dims), out_shape=outs, in_specs=...  7.12 us

profile of v2, /device:TPU:1, one launch (start us, length us, event | category | flops | bytes accessed | tf_op | source)
XLA Modules:
  0.0 55.9 jit_solution(13807189664468716122)
XLA Ops:
  1.3 47.4 %tile_and_reduce.1 = (bf16[256,2048]{1,0:T(8,128)(2,1)}, f32[8,896]{1,0:T(8,128)}, f32[8,768]{1,0:T(8,128)}, f32[16,128]{1,0:T(8,128)}) custom-call(bf16[64,256,128]{2,1,0:T(8,128)(2,1)} %pair_hbm.1, bf16[12,128]{1,0:T(8,128)(2,1)} %bitcast.20, f32[1,12]{1,0:T(1,128)} %bitcast.22, f32[64,192]{1,0:T(8,128)} %bitcast.18, f32[192,256]{1,0:T(8,128)} %k_ref.1, ...), custom_call_target="tpu_custom_call" | custom-call | tf_op jit(solution)/shard_map/tile_and_reduce/pallas_call | solution.py:700
  48.7 7.1 %pair_and_frames.1 = (bf16[64,256,128]{2,1,0:T(8,128)(2,1)}, f32[8,192]{1,0:T(8,128)}, f32[3,8,48]{2,1,0:T(8,128)}, f32[3,4,8]{2,1,0:T(4,128)}, f32[8,192]{1,0:T...) custom-call(bf16[256,2048]{1,0:T(8,128)(2,1)} %get-tuple-element.26., ...), custom_call_target="tpu_custom_call" | custom-call | tf_op jit(solution)/shard_map/pair_and_frames/pallas_call | solution.py:783

commit v3 on v2

--- a/solution.py
+++ b/solution.py
@@ -125,7 +125,7 @@
     go_ref,
     gpt_ref,
     gpair_ref,
-    ab_out,
+    pair_out,
     kfin_ref,
     qfin_ref,
     wfin_ref,
@@ -145,6 +145,8 @@
     g_s,
     p_s,
     pr_s,
+    bias_s,
+    ab_s,
     rhs_s,
     dh_s,
     dl_s,
@@ -159,13 +161,13 @@
     s0_s,
     sc0_s,
     s1_s,
-    sz_s,
+    sy_s,
     s2_s,
     sr_s,
     v0_s,
     vc0_s,
     v1_s,
-    vy_s,
+    vz_s,
     v2_s,
     vr_s,
     qx_s,
@@ -178,6 +180,7 @@
     wy_s,
     wr_s,
     pair_sem,
+    out_sem,
     send_sem,
     recv_sem,
 ):
@@ -243,8 +246,8 @@
     qf_s[0:F_PT] = jnp.transpose(q_ref[...])
     for a in range(3):
         qf_s[F_PT + 48 * a : F_PT + 48 * (a + 1)] = qg[a]
-    qf_s[F_N1:F_N2] = jnp.ones((HP, ni), F32)
-    qf_s[F_N2 : F_N2 + HP] = jnp.dot(
+    qf_s[F_N2 : F_N2 + HP] = jnp.ones((HP, ni), F32)
+    qf_s[F_N1:F_N2] = jnp.dot(
         norm_sel, qg[0] * qg[0] + qg[1] * qg[1] + qg[2] * qg[2], precision=HIGHEST
     )
     qf_s[F_N2 + HP :] = jnp.zeros((F_ALL - F_N2 - HP, ni), F32)
@@ -258,10 +261,10 @@
     kf_s[0:F_PT] = k_ref[...]
     for a in range(3):
         kf_s[F_PT + 48 * a : F_PT + 48 * (a + 1)] = kg[a]
-    kf_s[F_N1:F_N2] = jnp.dot(
+    kf_s[F_N2 : F_N2 + HP] = jnp.dot(
         norm_sel, kg[0] * kg[0] + kg[1] * kg[1] + kg[2] * kg[2], precision=HIGHEST
     )
-    kf_s[F_N2 : F_N2 + HP] = jnp.ones((HP, nj), F32)
+    kf_s[F_N1:F_N2] = jnp.ones((HP, nj), F32)
     kf_s[F_N2 + HP :] = jnp.zeros((F_ALL - F_N2 - HP, nj), F32)
     vf_s[0:G_PT] = v_ref[...]
     for a in range(3):
@@ -324,9 +327,9 @@
     count = count_ref[0]
 
     def forward(n, _):
-        logits = mm(kcat_s[...], qcat_s[:, tile(n, 256)])
-        prod = mm(vcat_s[...], gcat_s[:, tile(n, 256)])
-        biases, prods = [], []
+        t = tile(n, 256)
+        p_s[:, t] = mm(kcat_s[...], qcat_s[:, t])
+        pr_s[:, t] = mm(vcat_s[...], gcat_s[:, t])
         for half in range(2):
             g = 2 * n + half
             pltpu.make_async_copy(
@@ -340,18 +343,30 @@
                 two = jnp.concatenate([pair_v[8 * g + 2 * b], pair_v[8 * g + 2 * b + 1]], axis=1)
                 part = mm_nt(two, rhs_s[:, 256 * b : 256 * (b + 1)])
                 acc = part if acc is None else acc + part
-            biases.append(acc[:, :128])
-            prods.append(acc[:, 128:])
-        logits = logits + WL * jnp.concatenate(biases, axis=1)
-        prod = prod + jnp.concatenate(prods, axis=1)
-        valid = iota((nj, 256), 0) + col * nj < count
-        logits = jnp.where(valid, logits, -1000000000.0)
-        peak = jnp.max(logits, axis=0, keepdims=True)
-        e = jnp.exp(logits - peak)
-        p_s[:, tile(n, 256)] = e
-        pr_s[:, tile(n, 256)] = prod
-        total = jnp.sum(e, axis=0, keepdims=True)
-        upper = jnp.sum(e * prod, axis=0, keepdims=True)
+            bias_s[half] = acc
+        first = col * nj
+        peak = jnp.full((8, 256), -jnp.inf, F32)
+        for b in range(0, nj, 32):
+            rows = slice(b, b + 32)
+            bias = jnp.concatenate([bias_s[0, rows, :128], bias_s[1, rows, :128]], axis=1)
+            logits = p_s[rows, t] + WL * bias
+            logits = jnp.where(iota((32, 256), 0) + (first + b) < count, logits, -1000000000.0)
+            p_s[rows, t] = logits
+            peak = jnp.maximum(peak, jnp.max(logits.reshape(4, 8, 256), axis=0))
+        peak = jnp.max(peak, axis=0, keepdims=True)
+        total = jnp.zeros((8, 256), F32)
+        upper = jnp.zeros((8, 256), F32)
+        for b in range(0, nj, 32):
+            rows = slice(b, b + 32)
+            more = jnp.concatenate([bias_s[0, rows, 128:], bias_s[1, rows, 128:]], axis=1)
+            prod = pr_s[rows, t] + more
+            e = jnp.exp(p_s[rows, t] - peak)
+            pr_s[rows, t] = prod
+            p_s[rows, t] = e
+            total += jnp.sum(e.reshape(4, 8, 256), axis=0)
+            upper += jnp.sum((e * prod).reshape(4, 8, 256), axis=0)
+        total = jnp.sum(total, axis=0, keepdims=True)
+        upper = jnp.sum(upper, axis=0, keepdims=True)
         for half in range(2):
             at = slice(128 * half, 128 * (half + 1))
             st_s[0, pl.ds(2 * n + half, 1), :] = peak[:, at]
@@ -391,8 +406,8 @@
         ah_s[:, tile(g, 128)] = a_hi
         al_s[:, tile(g, 128)] = a_lo
         scaled = WL * dlog
-        ab_out[:, pl.ds(pl.multiple_of(g * 256, 256), 128)] = scaled.astype(BF16)
-        ab_out[:, pl.ds(pl.multiple_of(g * 256 + 128, 128), 128)] = a_hi
+        ab_s[:, pl.ds(pl.multiple_of(g * 256, 256), 128)] = scaled.astype(BF16)
+        ab_s[:, pl.ds(pl.multiple_of(g * 256 + 128, 128), 128)] = a_hi
         turned = jnp.transpose(dlog).astype(BF16)
         for b in range(8):
             acc = acc + mm(turned[16 * b : 16 * (b + 1)], pair_v[8 * g + b])
@@ -446,71 +461,102 @@
 
     s_core.wait()
     s1_s[...] = s0_s[:, :, c] + sc0_s[...]
-    s_z = spread_to(s1_s, sz_s, "row_0", z, nz, lambda p: p)
+    s_y = spread_to(s1_s, sy_s, "row_1", y, ny, lambda p: (slice(None), p))
     v_core.wait()
     v1_s[...] = v0_s[:, :, c] + vc0_s[...]
-    v_y = spread_to(v1_s, vy_s, "row_1", y, ny, lambda p: (slice(None), p))
-
-    def query_side(n, acc):
-        at = tile(n, 256)
-        lane = iota((ni, 256), 1)
-        e = ((lane >> 4) + n * 16 == iota((ni, 256), 0)).astype(BF16)
-        outs = []
-        for parts, hi_ref, lo_ref, head_of, rows, first in (
-            (kparts_s, dh_s, dl_s, head_of_feature, F_ALL, 0),
+    settle(w_x, wx_s, wm_s, nx)
+    w_w = send(wm_s, wz_s, {"col_1": 1 - w})
+    v_z = spread_to(v1_s, vz_s, "row_0", z, nz, lambda p: p)
+
+    qslab = ni // (nx * 2)
+    first = used[0]
+    used[0] += nx - 1
+
+    def q_copy(r):
+        peer = lax.rem(x + r, nx)
+        return pltpu.make_async_remote_copy(
+            src_ref=qout_s.at[peer],
+            dst_ref=qx_s.at[r - 1],
+            send_sem=send_sem.at[first + r - 1],
+            recv_sem=recv_sem.at[first + r - 1],
+            device_id={"col_0": peer},
+            device_id_type=MESH,
+        )
+
+    def query_side(r, _):
+        owner = lax.rem(x + r, nx)
+        at = tile(owner, 256)
+        e = ((iota((16, 256), 1) >> 4) == iota((16, 256), 0)).astype(BF16)
+        his, los = [], []
+        for parts, hi_ref, lo_ref, head_of, rows, start in (
+            (kparts_s, dh_s, dl_s, head_of_feature, F_N2, 0),
             (vparts_s, ah_s, al_s, head_of_value_feature, G_END - G_PT, G_PT),
         ):
-            full = mm(parts[0], hi_ref[:, at]) + mm(parts[0], lo_ref[:, at])
-            full += mm(parts[1], hi_ref[:, at])
-            keep = head_of(iota((rows, 256), 0) + first) == (iota((rows, 256), 1) & 15)
+            full = mm(parts[0, 0:rows], hi_ref[:, at]) + mm(parts[0, 0:rows], lo_ref[:, at])
+            full += mm(parts[1, 0:rows], hi_ref[:, at])
+            keep = head_of(iota((rows, 256), 0) + start) == (iota((rows, 256), 1) & 15)
             hi, lo = split2(jnp.where(keep, full, 0.0))
-            outs.append(mm_nt(e, hi) + mm_nt(e, lo))
-        return acc[0] + outs[0], acc[1] + outs[1]
-
-    sums = (jnp.zeros((ni, F_ALL), F32), jnp.zeros((ni, G_END - G_PT), F32))
-    sums = lax.fori_loop(0, chunks // 2, query_side, sums)
-    settle(w_x, wx_s, wm_s, nx)
-    w_w = send(wm_s, wz_s, {"col_1": 1 - w})
-    q1, q2 = lax.fori_loop(chunks // 2, chunks, query_side, sums)
-    qslab = ni // (nx * 2)
-    qout_s[:, :, :, 0:F_ALL] = q1.reshape(nx, 2, qslab, F_ALL)
-    qout_s[:, :, :, F_ALL : F_ALL + G_END - G_PT] = q2.reshape(nx, 2, qslab, G_END - G_PT)
-    qout_s[:, :, :, F_ALL + G_END - G_PT :] = jnp.zeros(
-        (nx, 2, qslab, qout_s.shape[3] - F_ALL - G_END + G_PT), F32
-    )
-    q_x = spread_to(qout_s, qx_s, "col_0", x, nx, lambda p: p)
-
-    done(s_z)
-    s2_s[...] = add([s1_s[z]] + [sz_s[r] for r in range(nz - 1)])
-    s_y = spread_to(s2_s, sr_s, "row_1", y, ny, lambda p: p)
+            his.append(hi)
+            los.append(lo)
+        out = mm_nt(e, jnp.concatenate(his, axis=0)) + mm_nt(e, jnp.concatenate(los, axis=0))
+        qout_s[owner] = out.reshape(2, qslab, qout_s.shape[3])
+
+        @pl.when(r < nx)
+        def _():
+            q_copy(r).start()
+
+        return 0
+
+    lax.fori_loop(1, nx + 1, query_side, 0)
+
+    def copy_out(g):
+        at = pl.ds(pl.multiple_of(8 * g, 8), 8)
+        return pltpu.make_async_copy(pair_v.at[at], pair_out.at[at], out_sem.at[g])
+
+    def pair_group(g, _):
+        g_rows = g_s[tile(g, 128)]
+        for b in range(8):
+            rhs_s[128:256, 128 * b : 128 * (b + 1)] = pair_rows(g_rows, b)
+        for b in range(4):
+            two = mm(ab_s[:, tile(g, 256)], rhs_s[:, 256 * b : 256 * (b + 1)]).astype(BF16)
+            pair_v[8 * g + 2 * b] = two[:, :128]
+            pair_v[8 * g + 2 * b + 1] = two[:, 128:]
+        copy_out(g).start()
+        return 0
+
+    lax.fori_loop(0, groups // 2, pair_group, 0)
     w_w.wait()
     wm_s[...] = wm_s[...] + wz_s[...]
     w_c = send(wm_s, wc_s, {"row_2": 1 - c})
-    done(v_y)
-    v2_s[...] = add([v1_s[:, y]] + [vy_s[r] for r in range(ny - 1)])
-    v_z = spread_to(v2_s, vr_s, "row_0", z, nz, lambda p: p)
+    done(s_y)
+    s2_s[...] = add([s1_s[:, y]] + [sy_s[r] for r in range(ny - 1)])
+    s_z = spread_to(s2_s, sr_s, "row_0", z, nz, lambda p: p)
     w_c.wait()
     wm_s[...] = wm_s[...] + wc_s[...]
     w_y = share(wm_s, wy_s, "row_1", y, ny)
-    done(q_x)
+    done(v_z)
+    v2_s[...] = add([v1_s[z]] + [vz_s[r] for r in range(nz - 1)])
+    v_y = spread_to(v2_s, vr_s, "row_1", y, ny, lambda p: p)
+    done([q_copy(r) for r in range(1, nx)])
     qz_s[...] = add([qout_s[x]] + [qx_s[r] for r in range(nx - 1)])
     q_w = send(qz_s.at[1 - w], qr_s, {"col_1": 1 - w})
+    lax.fori_loop(groups // 2, groups, pair_group, 0)
     settle(w_y, wy_s, wm_s, ny)
     w_z = share(wm_s, wr_s, "row_0", z, nz)
-    done(s_y)
-    kfin_ref[:, 0:F_ALL] = add([s2_s[y]] + [sr_s[r] for r in range(ny - 1)])
-    done(v_z)
-    kfin_ref[:, F_ALL:] = add([v2_s[z]] + [vr_s[r] for r in range(nz - 1)])
+    done(s_z)
+    kfin_ref[:, 0:F_ALL] = add([s2_s[z]] + [sr_s[r] for r in range(nz - 1)])
+    done(v_y)
+    kfin_ref[:, F_ALL:] = add([v2_s[y]] + [vr_s[r] for r in range(ny - 1)])
     q_w.wait()
     qfin_ref[...] = qz_s[w] + qr_s[...]
     settle(w_z, wr_s, wfin_ref, nz)
+    for g in range(groups):
+        copy_out(g).wait()
 
 
 def finish(
     dims,
-    ab_ref,
-    gpair_ref,
-    bw_ref,
+    pair_in,
     hw_ref,
     kfin_ref,
     qfin_ref,
@@ -532,12 +578,10 @@
     kf_out,
     w_out,
     hw_out,
-    g_s,
-    w_s,
     t_s,
-    rhs_s,
     pair_v,
-    pair_sem,
+    in_sem,
+    out_sem,
 ):
     nz, ny, nx, ni, nj = dims
     z, y, c = lax.axis_index("row_0"), lax.axis_index("row_1"), lax.axis_index("row_2")
@@ -547,33 +591,16 @@
     slab = nj // (nz * ny * 2)
     qslab = ni // (nx * 2)
 
-    w_s[...] = jnp.zeros((HP, 128), F32)
-    w_s[0:H] = bw_ref[...].astype(F32)
-    w_rows = jnp.concatenate([w_s[...]] * 8, axis=0)
-    for b in range(8):
-        rhs_s[0:128, 128 * b : 128 * (b + 1)] = pair_rows(w_rows, b)
-    g_s[...] = jnp.zeros(g_s.shape, F32)
-    for b in range(H):
-        g_s[pl.ds(b, ni, stride=HP), :] = gpair_ref[b].astype(F32)
-
-    def copy_out(g):
-        at = pl.ds(pl.multiple_of(8 * g, 8), 8)
-        return pltpu.make_async_copy(pair_v.at[at], pair_out.at[at], pair_sem.at[g])
-
     groups = ni // 8
 
-    def pair_group(g, _):
-        g_rows = g_s[tile(g, 128)]
-        for b in range(8):
-            rhs_s[128:256, 128 * b : 128 * (b + 1)] = pair_rows(g_rows, b)
-        for b in range(4):
-            two = mm(ab_ref[:, tile(g, 256)], rhs_s[:, 256 * b : 256 * (b + 1)]).astype(BF16)
-            pair_v[8 * g + 2 * b] = two[:, :128]
-            pair_v[8 * g + 2 * b + 1] = two[:, 128:]
-        copy_out(g).start()
-        return 0
-
-    lax.fori_loop(0, groups, pair_group, 0)
+    def part(g, src, dst, sem):
+        return pltpu.make_async_copy(src.at[pl.ds(8 * g, 8)], dst.at[pl.ds(8 * g, 8)], sem.at[g])
+
+    for g in range(groups):
+        part(g, pair_in, pair_v, in_sem).start()
+    for g in range(groups):
+        part(g, pair_in, pair_v, in_sem).wait()
+        part(g, pair_v, pair_out, out_sem).start()
 
     def exact(a, b):
         return jnp.dot(a, b, precision=HIGHEST)
@@ -621,11 +648,11 @@
     kg = rotate(rot, kp, shift)
     k_out[...] = (WL * WS) * kfin_ref[:, 0:F_PT]
     v_out[...] = kfin_ref[:, F_ALL : F_ALL + G_PT]
-    sums = exact(kfin_ref[:, F_N1:F_N2], expand)
+    sums = exact(kfin_ref[:, F_N2 : F_N2 + HP], expand)
     dkg = []
     for a in range(3):
-        part = kfin_ref[:, F_PT + 48 * a : F_PT + 48 * (a + 1)]
-        dkg.append(2.0 * coef * (part - kg[a] * sums))
+        piece = kfin_ref[:, F_PT + 48 * a : F_PT + 48 * (a + 1)]
+        dkg.append(2.0 * coef * (piece - kg[a] * sums))
     v_at = F_ALL + G_PT
     dvg = [kfin_ref[:, v_at + 96 * a : v_at + 96 * (a + 1)] for a in range(3)]
     for b, (dk, dv) in enumerate(zip(back(rot, dkg), back(rot, dvg))):
@@ -654,12 +681,12 @@
     qg = rotate(rot, qp, shift)
     gg = rotate(rot, gp)
     q_out[...] = (WL * WS) * qfin_ref[:, 0:F_PT]
-    sums = exact(qfin_ref[:, F_N2 : F_N2 + HP], expand)
+    sums = exact(qfin_ref[:, F_N1:F_N2], expand)
     dqg = []
     for a in range(3):
-        part = qfin_ref[:, F_PT + 48 * a : F_PT + 48 * (a + 1)]
-        dqg.append(-2.0 * coef * (qg[a] * sums - part))
-    opt = [qfin_ref[:, F_ALL + 96 * a : F_ALL + 96 * (a + 1)] - shift[a] for a in range(3)]
+        piece = qfin_ref[:, F_PT + 48 * a : F_PT + 48 * (a + 1)]
+        dqg.append(-2.0 * coef * (qg[a] * sums - piece))
+    opt = [qfin_ref[:, F_N2 + 96 * a : F_N2 + 96 * (a + 1)] - shift[a] for a in range(3)]
     for b, dq in enumerate(back(rot, dqg)):
         qp_out[b] = dq
     cols = []
@@ -678,7 +705,7 @@
     hw_out[...] = total[:, 0:H] / (softplus(hw) * (1.0 + jnp.exp(-hw)))
 
     for g in range(groups):
-        copy_out(g).wait()
+        part(g, pair_v, pair_out, out_sem).wait()
 
 
 def per_device(dims, *args):
@@ -690,23 +717,23 @@
     gpair = jnp.transpose(gpair, (1, 0, 2))
     lanes = ni * HP
     slab, qslab = nj // (nz * ny * 2), ni // (nx * 2)
-    kw, qw = F_ALL + G_ALL, 768
+    kw, qw = F_ALL + G_ALL, F_N2 + G_END - G_PT
     groups = lanes // 128
     sends = 3 * nx + 3 * (ny - 1) + 3 * (nz - 1) + 3
 
     def buf(*shape, dtype=F32):
         return pltpu.VMEM(shape, dtype)
 
-    ab, kfin, qfin, wfin = pl.pallas_call(
+    pair_grad, kfin, qfin, wfin = pl.pallas_call(
         functools.partial(mega, dims),
         out_shape=[
-            jax.ShapeDtypeStruct((nj, 2 * lanes), BF16),
+            jax.ShapeDtypeStruct((ni, nj, CZ), BF16),
             jax.ShapeDtypeStruct((slab, kw), F32),
             jax.ShapeDtypeStruct((qslab, qw), F32),
             jax.ShapeDtypeStruct((HP, 128), F32),
         ],
         in_specs=[ANY] + [VMEM] * 10 + [SMEM] + [VMEM] * 3,
-        out_specs=[VMEM] * 4,
+        out_specs=[ANY] + [VMEM] * 3,
         scratch_shapes=[
             buf(ni, nj, CZ, dtype=BF16),
             buf(F_ALL, ni),
@@ -724,6 +751,8 @@
             buf(lanes, 128),
             buf(nj, lanes),
             buf(nj, lanes),
+            buf(2, nj, 256),
+            buf(nj, 2 * lanes, dtype=BF16),
             buf(256, 1024, dtype=BF16),
             buf(nj, lanes, dtype=BF16),
             buf(nj, lanes, dtype=BF16),
@@ -738,15 +767,15 @@
             buf(nz, ny, 2, slab, F_ALL),
             buf(nz, ny, slab, F_ALL),
             buf(nz, ny, slab, F_ALL),
-            buf(nz - 1, ny, slab, F_ALL),
-            buf(ny, slab, F_ALL),
-            buf(ny - 1, slab, F_ALL),
+            buf(ny - 1, nz, slab, F_ALL),
+            buf(nz, slab, F_ALL),
+            buf(nz - 1, slab, F_ALL),
             buf(nz, ny, 2, slab, G_ALL),
             buf(nz, ny, slab, G_ALL),
             buf(nz, ny, slab, G_ALL),
-            buf(ny - 1, nz, slab, G_ALL),
-            buf(nz, slab, G_ALL),
-            buf(nz - 1, slab, G_ALL),
+            buf(nz - 1, ny, slab, G_ALL),
+            buf(ny, slab, G_ALL),
+            buf(ny - 1, slab, G_ALL),
             buf(nx - 1, 2, qslab, qw),
             buf(2, qslab, qw),
             buf(qslab, qw),
@@ -756,6 +785,7 @@
             buf(HP, 128),
             buf(ny, HP, 128),
             buf(nz, HP, 128),
+            pltpu.SemaphoreType.DMA((groups,)),
             pltpu.SemaphoreType.DMA((groups,)),
             pltpu.SemaphoreType.DMA((sends,)),
             pltpu.SemaphoreType.DMA((sends,)),
@@ -779,23 +809,21 @@
         jax.ShapeDtypeStruct((H, CZ), F32),
         jax.ShapeDtypeStruct((1, H), F32),
     ]
-    small = [bw, hw, kfin, qfin, wfin, qp, kp, vp, rot, tr, gpt]
+    small = [hw, kfin, qfin, wfin, qp, kp, vp, rot, tr, gpt]
     res = pl.pallas_call(
         functools.partial(finish, dims),
         out_shape=outs,
-        in_specs=[VMEM] * 13,
+        in_specs=[ANY] + [VMEM] * 10,
         out_specs=[ANY] + [VMEM] * 10,
         scratch_shapes=[
-            buf(lanes, 128),
-            buf(HP, 128),
             buf(512, 128),
-            buf(256, 1024, dtype=BF16),
             buf(ni, nj, CZ, dtype=BF16),
+            pltpu.SemaphoreType.DMA((groups,)),
             pltpu.SemaphoreType.DMA((groups,)),
         ],
         compiler_params=pltpu.CompilerParams(vmem_limit_bytes=60 * 2**20),
         name="pair_and_frames",
-    )(ab, gpair, *small)
+    )(pair_grad, *small)
     pair_grad, dq, dqp, dqf, dk, dv, dkp, dvp, dkf, dw, dhw = res
     turn = functools.partial(jnp.transpose, axes=(0, 2, 1))
     return pair_grad, dq.T, turn(dqp), dqf, dk.T, dv.T, turn(dkp), turn(dvp), dkf, dw.T, dhw[0]

time: 56 us -> 55.2 us (0.986)
  Pallas kernels: 54.6 us -> 53.4 us
    pallas_call x1, Pallas kernels: 47.4 us -> 46.1 us  [per_device(): pl.pallas_call(functools.partial(mega, dims), out_shape=[jax.ShapeDtypeSt...]
where the time goes in v3:
time: 55.2 us; the launch traced here: 54.7 us
  Pallas kernels  53.4 us (97%)
  between operations  1.3 us (2%)
    pallas_call x1, Pallas kernels, per_device(): pl.pallas_call(functools.partial(mega, dims), out_shape=[jax.ShapeDtypeSt...  46.1 us
    pallas_call x1, Pallas kernels, per_device(): pl.pallas_call(functools.partial(finish, dims), out_shape=outs, in_specs=...  7.23 us

profile of v3, /device:TPU:1, one launch (start us, length us, event | category | flops | bytes accessed | tf_op | source)
XLA Modules:
  0.0 54.7 jit_solution(6226825894728942757)
XLA Ops:
  1.3 46.1 %tile_and_reduce.1 = (bf16[64,256,128]{2,1,0:T(8,128)(2,1)}, f32[8,896]{1,0:T(8,128)}, f32[8,640]{1,0:T(8,128)}, f32[16,128]{1,0:T(8,128)}) custom-call(bf16[64,256,128]{2,1,0:T(8,128)(2,1)} %pair_hbm.1, bf16[12,128]{1,0:T(8,128)(2,1)} %bitcast.19, f32[1,12]{1,0:T(1,128)} %bitcast.20, f32[64,192]{1,0:T(8,128)} %bitcast.17, f32[192,256]{1,0:T(8,128)} %k_ref.1, ...), custom_call_target="tpu_custom_call" | custom-call | tf_op jit(solution)/shard_map/tile_and_reduce/pallas_call | solution.py:727
  47.4 7.2 %pair_and_frames.1 = (bf16[64,256,128]{2,1,0:T(8,128)(2,1)}, f32[8,192]{1,0:T(8,128)}, f32[3,8,48]{2,1,0:T(8,128)}, f32[3,4,8]{2,1,0:T(4,128)}, f32[8,192]{1,0:T...) custom-call(bf16[64,256,128]{2,1,0:T(8,128)(2,1)} %get-tuple-element, ...), custom_call_target="tpu_custom_call" | custom-call | tf_op jit(solution)/shard_map/pair_and_frames/pallas_call | solution.py:813

commit v4 on v3

--- a/solution.py
+++ b/solution.py
@@ -161,13 +161,13 @@
     s0_s,
     sc0_s,
     s1_s,
-    sy_s,
+    sa_s,
     s2_s,
     sr_s,
     v0_s,
     vc0_s,
     v1_s,
-    vz_s,
+    va_s,
     v2_s,
     vr_s,
     qx_s,
@@ -451,7 +451,7 @@
         done(copies)
         dst[...] = add([slots[n] for n in range(count)])
 
-    w_x = share(wm_s, wx_s, "col_0", x, nx)
+    w_c = send(wm_s, wc_s, {"row_2": 1 - c})
 
     aout = mm_nt(ah_s[...], gcat_s[0:G_ALL])
     aout += mm_nt(ah_s[...], gcat_s[G_ALL : 2 * G_ALL])
@@ -459,15 +459,9 @@
     v0_s[...] = aout.reshape(v0_s.shape)
     v_core = send(v0_s.at[:, :, 1 - c], vc0_s, {"row_2": 1 - c})
 
-    s_core.wait()
-    s1_s[...] = s0_s[:, :, c] + sc0_s[...]
-    s_y = spread_to(s1_s, sy_s, "row_1", y, ny, lambda p: (slice(None), p))
-    v_core.wait()
-    v1_s[...] = v0_s[:, :, c] + vc0_s[...]
-    settle(w_x, wx_s, wm_s, nx)
-    w_w = send(wm_s, wz_s, {"col_1": 1 - w})
-    v_z = spread_to(v1_s, vz_s, "row_0", z, nz, lambda p: p)
-
+    w_c.wait()
+    wm_s[...] = wm_s[...] + wc_s[...]
+    w_x = share(wm_s, wx_s, "col_0", x, nx)
     qslab = ni // (nx * 2)
     first = used[0]
     used[0] += nx - 1
@@ -507,7 +501,17 @@
 
         return 0
 
-    lax.fori_loop(1, nx + 1, query_side, 0)
+    lax.fori_loop(1, 1 + nx // 2, query_side, 0)
+    s_core.wait()
+    s1_s[...] = s0_s[:, :, c] + sc0_s[...]
+    s_first = spread_to(s1_s, sa_s, "row_0", z, nz, lambda p: p)
+    v_core.wait()
+    v1_s[...] = v0_s[:, :, c] + vc0_s[...]
+    settle(w_x, wx_s, wm_s, nx)
+    w_w = send(wm_s, wz_s, {"col_1": 1 - w})
+    v_first = spread_to(v1_s, va_s, "row_1", y, ny, lambda p: (slice(None), p))
+
+    lax.fori_loop(1 + nx // 2, nx + 1, query_side, 0)
 
     def copy_out(g):
         at = pl.ds(pl.multiple_of(8 * g, 8), 8)
@@ -527,26 +531,23 @@
     lax.fori_loop(0, groups // 2, pair_group, 0)
     w_w.wait()
     wm_s[...] = wm_s[...] + wz_s[...]
-    w_c = send(wm_s, wc_s, {"row_2": 1 - c})
-    done(s_y)
-    s2_s[...] = add([s1_s[:, y]] + [sy_s[r] for r in range(ny - 1)])
-    s_z = spread_to(s2_s, sr_s, "row_0", z, nz, lambda p: p)
-    w_c.wait()
-    wm_s[...] = wm_s[...] + wc_s[...]
     w_y = share(wm_s, wy_s, "row_1", y, ny)
-    done(v_z)
-    v2_s[...] = add([v1_s[z]] + [vz_s[r] for r in range(nz - 1)])
-    v_y = spread_to(v2_s, vr_s, "row_1", y, ny, lambda p: p)
+    done(s_first)
+    s2_s[...] = add([s1_s[z]] + [sa_s[r] for r in range(nz - 1)])
+    s_second = spread_to(s2_s, sr_s, "row_1", y, ny, lambda p: p)
+    done(v_first)
+    v2_s[...] = add([v1_s[:, y]] + [va_s[r] for r in range(ny - 1)])
+    v_second = spread_to(v2_s, vr_s, "row_0", z, nz, lambda p: p)
     done([q_copy(r) for r in range(1, nx)])
     qz_s[...] = add([qout_s[x]] + [qx_s[r] for r in range(nx - 1)])
     q_w = send(qz_s.at[1 - w], qr_s, {"col_1": 1 - w})
-    lax.fori_loop(groups // 2, groups, pair_group, 0)
     settle(w_y, wy_s, wm_s, ny)
     w_z = share(wm_s, wr_s, "row_0", z, nz)
-    done(s_z)
-    kfin_ref[:, 0:F_ALL] = add([s2_s[z]] + [sr_s[r] for r in range(nz - 1)])
-    done(v_y)
-    kfin_ref[:, F_ALL:] = add([v2_s[y]] + [vr_s[r] for r in range(ny - 1)])
+    lax.fori_loop(groups // 2, groups, pair_group, 0)
+    done(s_second)
+    kfin_ref[:, 0:F_ALL] = add([s2_s[y]] + [sr_s[r] for r in range(ny - 1)])
+    done(v_second)
+    kfin_ref[:, F_ALL:] = add([v2_s[z]] + [vr_s[r] for r in range(nz - 1)])
     q_w.wait()
     qfin_ref[...] = qz_s[w] + qr_s[...]
     settle(w_z, wr_s, wfin_ref, nz)
@@ -598,10 +599,6 @@
 
     for g in range(groups):
         part(g, pair_in, pair_v, in_sem).start()
-    for g in range(groups):
-        part(g, pair_in, pair_v, in_sem).wait()
-        part(g, pair_v, pair_out, out_sem).start()
-
     def exact(a, b):
         return jnp.dot(a, b, precision=HIGHEST)
 
@@ -663,6 +660,10 @@
         cols.append([over(dkg[a] * kp[b]) + over(dvg[a] * vp[b]) for b in range(3)])
         cols[a].append(over(dkg[a]) + over(dvg[a]))
     frame(kf_out, cols, slab)
+
+    for g in range(groups):
+        part(g, pair_in, pair_v, in_sem).wait()
+        part(g, pair_v, pair_out, out_sem).start()
 
     at = col * qslab
     base = tile(z * ny + y, 128)
@@ -767,15 +768,15 @@
             buf(nz, ny, 2, slab, F_ALL),
             buf(nz, ny, slab, F_ALL),
             buf(nz, ny, slab, F_ALL),
-            buf(ny - 1, nz, slab, F_ALL),
-            buf(nz, slab, F_ALL),
-            buf(nz - 1, slab, F_ALL),
+            buf(nz - 1, ny, slab, F_ALL),
+            buf(ny, slab, F_ALL),
+            buf(ny - 1, slab, F_ALL),
             buf(nz, ny, 2, slab, G_ALL),
             buf(nz, ny, slab, G_ALL),
             buf(nz, ny, slab, G_ALL),
-            buf(nz - 1, ny, slab, G_ALL),
-            buf(ny, slab, G_ALL),
-            buf(ny - 1, slab, G_ALL),
+            buf(ny - 1, nz, slab, G_ALL),
+            buf(nz, slab, G_ALL),
+            buf(nz - 1, slab, G_ALL),
             buf(nx - 1, 2, qslab, qw),
             buf(2, qslab, qw),
             buf(qslab, qw),

time: 55.2 us -> 53.2 us (0.964)
  Pallas kernels: 53.4 us -> 51.7 us
    pallas_call x1, Pallas kernels: 7.23 us -> 5.79 us  [per_device(): pl.pallas_call(functools.partial(finish, dims), out_shape=outs, in_specs=...]
where the time goes in v4:
time: 53.2 us; the launch traced here: 53 us
  Pallas kernels  51.7 us (97%)
  between operations  1.3 us (2%)
    pallas_call x1, Pallas kernels, per_device(): pl.pallas_call(functools.partial(mega, dims), out_shape=[jax.ShapeDtypeSt...  45.9 us
    pallas_call x1, Pallas kernels, per_device(): pl.pallas_call(functools.partial(finish, dims), out_shape=outs, in_specs=...  5.79 us

profile of v4, /device:TPU:1, one launch (start us, length us, event | category | flops | bytes accessed | tf_op | source)
XLA Modules:
  0.0 53.0 jit_solution(6628616235805387916)
XLA Ops:
  1.3 45.9 %tile_and_reduce.1 = (bf16[64,256,128]{2,1,0:T(8,128)(2,1)}, f32[8,896]{1,0:T(8,128)}, f32[8,640]{1,0:T(8,128)}, f32[16,128]{1,0:T(8,128)}) custom-call(bf16[64,256,128]{2,1,0:T(8,128)(2,1)} %pair_hbm.1, bf16[12,128]{1,0:T(8,128)(2,1)} %bitcast.19, f32[1,12]{1,0:T(1,128)} %bitcast.20, f32[64,192]{1,0:T(8,128)} %bitcast.17, f32[192,256]{1,0:T(8,128)} %k_ref.1, ...), custom_call_target="tpu_custom_call" | custom-call | tf_op jit(solution)/shard_map/tile_and_reduce/pallas_call | solution.py:728
  47.2 5.8 %pair_and_frames.1 = (bf16[64,256,128]{2,1,0:T(8,128)(2,1)}, f32[8,192]{1,0:T(8,128)}, f32[3,8,48]{2,1,0:T(8,128)}, f32[3,4,8]{2,1,0:T(4,128)}, f32[8,192]{1,0:T...) custom-call(bf16[64,256,128]{2,1,0:T(8,128)(2,1)} %get-tuple-element, ...), custom_call_target="tpu_custom_call" | custom-call | tf_op jit(solution)/shard_map/pair_and_frames/pallas_call | solution.py:814

commit v5 on v4

--- a/solution.py
+++ b/solution.py
@@ -507,9 +507,9 @@
     s_first = spread_to(s1_s, sa_s, "row_0", z, nz, lambda p: p)
     v_core.wait()
     v1_s[...] = v0_s[:, :, c] + vc0_s[...]
+    v_first = spread_to(v1_s, va_s, "row_1", y, ny, lambda p: (slice(None), p))
     settle(w_x, wx_s, wm_s, nx)
     w_w = send(wm_s, wz_s, {"col_1": 1 - w})
-    v_first = spread_to(v1_s, va_s, "row_1", y, ny, lambda p: (slice(None), p))
 
     lax.fori_loop(1 + nx // 2, nx + 1, query_side, 0)
 

time: 53.2 us -> 53.2 us (level)
  no operation moved by 1% of the time
where the time goes in v5:
time: 53.2 us; the launch traced here: 53 us
  Pallas kernels  51.7 us (97%)
  between operations  1.3 us (2%)
    pallas_call x1, Pallas kernels, per_device(): pl.pallas_call(functools.partial(mega, dims), out_shape=[jax.ShapeDtypeSt...  45.9 us
    pallas_call x1, Pallas kernels, per_device(): pl.pallas_call(functools.partial(finish, dims), out_shape=outs, in_specs=...  5.79 us

profile of v5, /device:TPU:1, one launch (start us, length us, event | category | flops | bytes accessed | tf_op | source)
XLA Modules:
  0.0 53.0 jit_solution(1992960902038230330)
XLA Ops:
  1.3 45.9 %tile_and_reduce.1 = (bf16[64,256,128]{2,1,0:T(8,128)(2,1)}, f32[8,896]{1,0:T(8,128)}, f32[8,640]{1,0:T(8,128)}, f32[16,128]{1,0:T(8,128)}) custom-call(bf16[64,256,128]{2,1,0:T(8,128)(2,1)} %pair_hbm.1, bf16[12,128]{1,0:T(8,128)(2,1)} %bitcast.19, f32[1,12]{1,0:T(1,128)} %bitcast.20, f32[64,192]{1,0:T(8,128)} %bitcast.17, f32[192,256]{1,0:T(8,128)} %k_ref.1, ...), custom_call_target="tpu_custom_call" | custom-call | tf_op jit(solution)/shard_map/tile_and_reduce/pallas_call | solution.py:728
  47.2 5.8 %pair_and_frames.1 = (bf16[64,256,128]{2,1,0:T(8,128)(2,1)}, f32[8,192]{1,0:T(8,128)}, f32[3,8,48]{2,1,0:T(8,128)}, f32[3,4,8]{2,1,0:T(4,128)}, f32[8,192]{1,0:T...) custom-call(bf16[64,256,128]{2,1,0:T(8,128)(2,1)} %get-tuple-element, ...), custom_call_target="tpu_custom_call" | custom-call | tf_op jit(solution)/shard_map/pair_and_frames/pallas_call | solution.py:814
